TPU v7x, 32 devices: a whole 2x2x4 slice. The times are simulated.
32 devices in a mesh: lat: 4 (over z), lon: 8 (over y, x, core).
Axes of the slice: x: 2, y: 2, z: 4, core: 2. Of those that a mesh axis runs over, the one named last changes fastest.
Arguments:
- zonal_wind: float32 [32, 32, 2048], P(None, 'lat', 'lon'), may hold values from -6 to 6
- merid_wind: float32 [32, 32, 2048], P(None, 'lat', 'lon'), may hold values from -6 to 6
- vertical_wind: float32 [32, 32, 2048], P(None, 'lat', 'lon'), may hold values from -6 to 6
- pressure: float32 [32, 32, 2048], P(None, 'lat', 'lon'), may hold values from -6 to 6
- zonal_coef: float32 [32], P('lat'), may hold values from 0.05 to 0.4
- merid_coef: float32 [32], P('lat'), may hold values from 0.05 to 0.4
- level_coef: float32 [32], replicated, may hold values from 0.3 to 1.5
- sound_coef: float32 [32, 32, 2048], P(None, 'lat', 'lon'), may hold values from 0.2 to 2
- cutoff: int32 [32], replicated, may hold values from 1 to 511
- filter_mask: int32 [32], replicated, may hold values from 0 to 1, as said below
Outputs:
- zonal_next: float32 [32, 32, 2048], P(None, 'lat', 'lon')
- merid_next: float32 [32, 32, 2048], P(None, 'lat', 'lon')
- vertical_next: float32 [32, 32, 2048], P(None, 'lat', 'lon')
- pressure_next: float32 [32, 32, 2048], P(None, 'lat', 'lon')
Inputs may be any that keep to these rules, and one draw needn't show every extreme that they name: `filter_mask`: for every latitude j below 16 exactly one of j and j + 16 is filtered; the filtered ones are the first n and the last 16 - n latitudes, for some n from 4 to 12.
All inputs are finite; a program needn't handle non-finite values.
Results may differ from a plain program's by a relative error of at most 0.0001.
Values sent between devices are 32-bit elements; how exact they have to be, the bound alone decides.
A program may use at most 64 MiB of HBM per device.

v0:
```python
import math

import jax
import jax.numpy as jnp
from jax import lax
from jax.sharding import PartitionSpec as P

SUBSTEPS = 2


def extended(block, sides, width):
    for axis, dim in sides:
        count = lax.axis_size(axis)
        forward = [(i, i + 1) for i in range(count - 1)]
        forward.append((count - 1, 0))
        backward = [(target, source) for source, target in forward]
        low = lax.ppermute(
            lax.slice_in_dim(block, block.shape[dim] - width, None, axis=dim), axis, forward
        )
        high = lax.ppermute(lax.slice_in_dim(block, 0, width, axis=dim), axis, backward)
        block = jnp.concatenate([low, block, high], axis=dim)
    return block


def rim_fix(padded, lat_dim):
    band_index = lax.axis_index("lat")
    bands = lax.axis_size("lat")
    extent = padded.shape[lat_dim]
    position = lax.broadcasted_iota(jnp.int32, padded.shape, lat_dim)
    first_edge = jnp.logical_and(position == 0, band_index == 0)
    final_edge = jnp.logical_and(position == extent - 1, band_index == bands - 1)
    return jnp.where(jnp.logical_or(first_edge, final_edge), 0.0, padded)


def dft_tables(length):
    half_len = length // 2
    sample = lax.broadcasted_iota(jnp.int32, (length, length), 0)
    column = lax.broadcasted_iota(jnp.int32, (length, length), 1)
    is_cosine = column <= half_len
    wavenum = jnp.where(is_cosine, column, column - half_len)
    phase = sample * wavenum % length
    angle = 2.0 * math.pi / length * phase.astype(jnp.float32)
    forward = jnp.where(is_cosine, jnp.cos(angle), jnp.sin(angle))
    single = jnp.logical_and(is_cosine, jnp.logical_or(wavenum == 0, wavenum == half_len))
    weight = jnp.where(single, 1.0, 2.0) / length
    inverse = jnp.transpose(forward * weight)
    wave_row = wavenum[0].astype(jnp.float32)
    return (forward, inverse, wave_row)


def damping(wave_row, limits):
    bound_col = limits[:, None]
    ratio = bound_col / jnp.maximum(wave_row[None, :], 1.0)
    return jnp.where(wave_row[None, :] > bound_col, ratio * ratio, 1.0)


def transform_band(block, limits, forward, inverse, wave_row):
    circles = lax.all_to_all(block, "lon", split_axis=1, concat_axis=3, tiled=True)
    spectra = jnp.einsum("vetj,jc->vetc", circles, forward, precision=lax.Precision.HIGHEST)
    scaled = spectra * damping(wave_row, limits)
    damped = jnp.einsum("vetc,cj->vetj", scaled, inverse, precision=lax.Precision.HIGHEST)
    return lax.all_to_all(damped, "lon", split_axis=3, concat_axis=1, tiled=True)


def filtered_increments(increments, own_flags, own_limits, forward, inverse, wave_row):
    flag_cols = own_flags[:, None]
    damped = transform_band(increments, own_limits, forward, inverse, wave_row)
    return jnp.where(flag_cols, damped, increments)


def column_solve(vertical_wind, pstar, level_coef, sound_coef):
    levels = vertical_wind.shape[0]
    zero_slab = jnp.zeros_like(vertical_wind[0])
    ratios = []
    values = []
    prev_ratio = zero_slab
    prev_value = zero_slab
    for level in range(levels):
        alpha = level_coef[level]
        below = alpha * sound_coef[level]
        if level + 1 < levels:
            above = alpha * sound_coef[level + 1]
            rhs = vertical_wind[level] - alpha * (pstar[level + 1] - pstar[level])
        else:
            above = zero_slab
            rhs = vertical_wind[level] + alpha * pstar[level]
        pivot = 1.0 + below + above + below * prev_ratio
        prev_ratio = -above / pivot
        prev_value = (rhs + below * prev_value) / pivot
        ratios.append(prev_ratio)
        values.append(prev_value)
    solved = [zero_slab] * levels
    upper_value = values[levels - 1]
    solved[levels - 1] = upper_value
    for level in range(levels - 2, -1, -1):
        upper_value = values[level] - ratios[level] * upper_value
        solved[level] = upper_value
    new_wind = jnp.stack(solved)
    wind_below = jnp.concatenate([zero_slab[None], new_wind[:-1]], axis=0)
    new_pressure = pstar - sound_coef * (new_wind - wind_below)
    return (new_wind, new_pressure)


def body(
    zonal_wind,
    merid_wind,
    vertical_wind,
    pressure,
    zonal_coef,
    merid_coef,
    level_coef,
    sound_coef,
    cutoff,
    filter_mask,
):
    lat_rows = pressure.shape[1]
    start = lax.axis_index("lat") * lat_rows
    own_flags = lax.dynamic_slice_in_dim(filter_mask, start, lat_rows) > 0
    own_limits = lax.dynamic_slice_in_dim(cutoff, start, lat_rows).astype(jnp.float32)
    forward, inverse, wave_row = dft_tables(pressure.shape[2] * lax.axis_size("lon"))
    zonal_rows = zonal_coef[None, :, None]
    merid_rows = merid_coef[None, :, None]
    for step in range(SUBSTEPS):
        padded = extended(pressure, (("lat", 1), ("lon", 2)), 1)
        padded = rim_fix(padded, 1)
        zonal_step = -zonal_rows * (padded[:, 1:-1, 2:] - padded[:, 1:-1, :-2])
        merid_step = -merid_rows * (padded[:, 2:, 1:-1] - padded[:, :-2, 1:-1])
        increments = jnp.stack([zonal_step, merid_step])
        damped = filtered_increments(increments, own_flags, own_limits, forward, inverse, wave_row)
        winds = jnp.stack([zonal_wind, merid_wind]) + damped
        wind_pad = extended(winds, (("lat", 2), ("lon", 3)), 1)
        wind_pad = rim_fix(wind_pad, 2)
        diverge = zonal_rows * (wind_pad[0, :, 1:-1, 2:] - wind_pad[0, :, 1:-1, :-2])
        diverge = diverge + merid_rows * (wind_pad[1, :, 2:, 1:-1] - wind_pad[1, :, :-2, 1:-1])
        pstar = pressure - sound_coef * diverge
        vertical_wind, pressure = column_solve(vertical_wind, pstar, level_coef, sound_coef)
        zonal_wind = winds[0]
        merid_wind = winds[1]
    return (zonal_wind, merid_wind, vertical_wind, pressure)


def solution(mesh):
    in_specs = (
        P(None, "lat", "lon"),
        P(None, "lat", "lon"),
        P(None, "lat", "lon"),
        P(None, "lat", "lon"),
        P("lat"),
        P("lat"),
        P(),
        P(None, "lat", "lon"),
        P(),
        P(),
    )
    out_specs = (
        P(None, "lat", "lon"),
        P(None, "lat", "lon"),
        P(None, "lat", "lon"),
        P(None, "lat", "lon"),
    )
    return jax.shard_map(body, mesh=mesh, in_specs=in_specs, out_specs=out_specs, check_vma=False)
```

profile of v0, /device:TPU:0, one launch (start us, length us, event | category | flops | bytes accessed | tf_op | source)
XLA Modules:
  0.0 585.0 jit_solution(11969171518378575389)
XLA Ops:
  0.7 1.1 fusion.87
  1.8 5.1 collective-permute-start.1
  7.0 2.1 iota_select_fusion
  9.1 3.5 collective-permute-done
  13.5 6.0 %collective-permute-done.3 = f32[32,10,1]{2,1,0:T(8,128)S(1)} collective-permute-done((f32[32,10,1]{2,1,0:T(8,128)S(1)}, f32[32,10,1]{2,1,0:T(8,128)S(1)}, u32[]{:S(2)}, u32[]{:S(2)}) %collective-permute-start.3) | collective-permute-done | bytes 1312 | tf_op jit(solution)/shard_map/ppermute | solution.py:20
  19.5 3.0 collective-permute-done.2
  24.2 3.8 all-to-all-start
  28.2 9.5 %all-to-all-done = f32[2,32,8,256]{3,2,0,1:T(8,128)S(1)} async-done(((f32[2,32,8,256]{3,2,0,1:T(8,128)}), f32[2,32,8,256]{3,2,0,1:T(8,128)S(1)}, u32[]{:S(2)}, u32[]{:S(2)}) %all-to-all-start) | async-done | bytes 524320 | tf_op jit(solution)/shard_map/all_to_all | solution.py:58
  38.0 75.8 %fusion.15 = f32[2,4,8,2048]{3,2,1,0:T(8,128)S(1)} fusion(f32[2,4,8,2048]{3,2,1,0:T(8,128)S(1)} %all_to_all.55, s32[2048]{0:T(1024)S(1)} %iota_add_fusion, pred[2048]{0:T(1024)(128)(4,1)S(1)} %iota_compare_fusion, f32[8,2048]{1,0:T(8,128)S(1)} %fusion.44), kind=kOutput, calls=%fused_computation.21 | convolution fusion | flops 3288465408 | bytes 1124352 | tf_op jit(solution)/shard_map/vetj,jc->vetc/dot_general | solution.py:59
  113.9 82.4 %fusion.5 = f32[2,4,8,2048]{3,2,1,0:T(8,128)S(1)} fusion(f32[2,4,8,2048]{3,2,1,0:T(8,128)S(1)} %fusion.15, s32[2048]{0:T(1024)S(1)} %iota_add_fusion, pred[2048]{0:T(1024)(128)(4,1)S(1)} %iota_compare_fusion), kind=kOutput, calls=%fused_computation.8 | convolution fusion | flops 3317694464 | bytes 1058816 | tf_op jit(solution)/shard_map/vetc,cj->vetj/dot_general | solution.py:61
  196.4 5.8 copy.23
  202.1 12.3 %reshape.77 = f32[8,1,16384]{2,1,0:T(1,128)} reshape(f32[2048,2,4,8]{3,2,1,0:T(4,128)} %bitcast.161) | data formatting | bytes 1048576
  214.4 3.6 all-to-all-start.1
  218.1 9.6 %all-to-all-done.1 = f32[8,1,16384]{2,1,0:T(1,128)S(1)} async-done(((f32[8,1,16384]{2,1,0:T(1,128)}), f32[8,1,16384]{2,1,0:T(1,128)S(1)}, u32[]{:S(2)}, u32[]{:S(2)}) %all-to-all-start.1) | async-done | bytes 524320 | tf_op jit(solution)/shard_map/all_to_all | solution.py:62
  228.2 1.9 reduce
  230.1 13.2 %reshape.78 = f32[2048,2,4,8]{3,2,1,0:T(4,128)} reshape(f32[8,16384]{1,0:T(8,128)S(1)} %reduce) | data formatting | bytes 1048576
  243.3 6.7 %copy.24 = f32[2,4,8,8,256]{4,2,0,1,3:T(8,128)S(1)} copy(f32[2,4,8,8,256]{2,1,0,4,3:T(4,128)} %bitcast.162) | data formatting | bytes 1048576 | tf_op jit(solution)/shard_map/all_to_all | solution.py:62
  250.6 1.7 collective-permute-start.4
  253.0 1.5 collective-permute-done.5
  254.5 2.1 collective-permute-done.4
  258.8 10.3 %collective-permute-done.7 = f32[2,32,10,1]{3,2,1,0:T(8,128)S(1)} collective-permute-done((f32[2,32,10,1]{3,2,1,0:T(8,128)S(1)}, f32[2,32,10,1]{3,2,1,0:T(8,128)S(1)}, u32[]{:S(2)}, u32[]{:S(2)}) %collective-permute-start.7) | collective-permute-done | bytes 2592 | tf_op jit(solution)/shard_map/ppermute | solution.py:20
  269.1 1.4 collective-permute-done.6
  270.5 1.2 maximum_select_fusion
  272.0 20.4 %add_divide_fusion.32 = (f32[1,8,256]{2,1,0:T(8,128)S(1)}, f32[1,8,256]{2,1,0:T(8,128)S(1)}, f32[1,8,256]{2,1,0:T(8,128)S(1)}, f32[1,8,256]{2,1,0:T(8,128)S(1)},...) fusion(f32[32,8,256]{2,1,0:T(8,128)S(1)} %copy-done.6, ...), kind=kLoop, calls=%fused_computation.313 | loop fusion | flops 882688 | bytes 1523836 | tf_op jit(solution)/shard_map/div | solution.py:89
  292.5 2.0 constant_dynamic-update-slice_fusion.62
  295.5 1.6 collective-permute-start.8
  297.2 2.2 collective-permute-done.9
  299.4 1.8 collective-permute-done.8
  302.0 5.6 collective-permute-done.11
  307.6 2.2 collective-permute-done.10
  311.4 12.3 %all_to_all.72 = f32[2,32,8,256]{3,2,0,1:T(8,128)S(1)} all-to-all(f32[2,32,8,256]{3,2,0,1:T(8,128)S(1)} %copy.29), channel_id=1, replica_groups=mesh['lat'=4,'lon'=8] {'lon'}, dimensions={1} | all-to-all | bytes 1048576 | tf_op jit(solution)/shard_map/all_to_all | solution.py:58
  325.0 77.2 %fusion.18 = f32[2,4,8,2048]{3,2,1,0:T(8,128)S(1)} fusion(f32[2,4,8,2048]{3,2,1,0:T(8,128)} %all_to_all.63, s32[2048]{0:T(1024)} %copy-done.21, pred[2048]{0:T(1024)(128)(4,1)} %copy-done.24, f32[8,2048]{1,0:T(8,128)} %copy-done.20), kind=kOutput, calls=%fused_computation.22 | convolution fusion | flops 3288465408 | bytes 1124352 | tf_op jit(solution)/shard_map/vetj,jc->vetc/dot_general | solution.py:59
  402.2 82.1 %fusion.3 = f32[2,4,8,2048]{3,2,1,0:T(8,128)S(1)} fusion(f32[2,4,8,2048]{3,2,1,0:T(8,128)S(1)} %fusion.18, s32[2048]{0:T(1024)S(1)} %copy-done.22, pred[2048]{0:T(1024)(128)(4,1)S(1)} %copy-done.25), kind=kOutput, calls=%fused_computation.6 | convolution fusion | flops 3317694464 | bytes 1058816 | tf_op jit(solution)/shard_map/vetc,cj->vetj/dot_general | solution.py:61
  484.3 5.8 copy.31
  490.1 11.6 %reshape.79 = f32[8,1,16384]{2,1,0:T(1,128)S(1)} reshape(f32[2048,2,4,8]{3,2,1,0:T(4,128)} %bitcast.163) | data formatting | bytes 1048576
  501.7 12.8 %all_to_all.73 = f32[8,1,16384]{2,1,0:T(1,128)} all-to-all(f32[8,1,16384]{2,1,0:T(1,128)S(1)} %reshape.79), channel_id=1, replica_groups=mesh['lat'=4,'lon'=8] {'lon'}, dimensions={0} | all-to-all | bytes 1048576 | tf_op jit(solution)/shard_map/all_to_all | solution.py:62
  514.5 2.9 reduce.1
  517.4 13.2 %reshape.80 = f32[2048,2,4,8]{3,2,1,0:T(4,128)} reshape(f32[8,16384]{1,0:T(8,128)S(1)} %reduce.1) | data formatting | bytes 1048576
  530.7 6.7 %copy.32 = f32[2,4,8,8,256]{4,2,1,3,0:T(8,128)S(1)} copy(f32[2,4,8,8,256]{2,1,0,4,3:T(4,128)} %bitcast.164) | data formatting | bytes 1048576 | tf_op jit(solution)/shard_map/all_to_all | solution.py:62
  538.7 1.7 collective-permute-start.12
  540.5 2.9 collective-permute-done.13
  543.4 1.4 collective-permute-done.12
  546.8 10.5 %collective-permute-done.15 = f32[2,32,10,1]{3,2,0,1:T(8,128)S(1)} collective-permute-done((f32[2,32,10,1]{3,2,0,1:T(8,128)S(1)}, f32[2,32,10,1]{3,2,0,1:T(8,128)S(1)}, u32[]{:S(2)}, u32[]{:S(2)}) %collective-permute-start.15) | collective-permute-done | bytes 2592 | tf_op jit(solution)/shard_map/ppermute | solution.py:20
  557.3 1.3 collective-permute-done.14
  558.6 1.8 maximum_select_fusion.1
  560.3 1.0 fusion.25
  561.3 20.7 %add_divide_fusion.1 = (f32[1,8,256]{2,1,0:T(8,128)S(1)}, f32[1,8,256]{2,1,0:T(8,128)S(1)}, f32[1,8,256]{2,1,0:T(8,128)S(1)}, f32[1,8,256]{2,1,0:T(8,128)S(1)}, ...) fusion(f32[1,8,256]{2,1,0:T(8,128)S(1)} %get-tuple-element.102,, ...), kind=kLoop, calls=%fused_computation.248 | loop fusion | flops 452608 | bytes 1269884 | tf_op jit(solution)/shard_map/div | solution.py:89
  582.0 1.5 constant_dynamic-update-slice_fusion.125
  (183 shorter events, 16.1 us)
Async XLA Ops:
  0.7 12.8 %copy-start.28 = (f32[8]{0:T(128)S(1)}, f32[8]{0:T(128)}, u32[]{:S(2)}) copy-start(f32[8]{0:T(128)} %param.15) | copy-start | bytes 100
  0.7 27.3 %copy-start.31 = (s32[32]{0:T(128)S(1)}, s32[32]{0:T(128)}, u32[]{:S(2)}) copy-start(s32[32]{0:T(128)} %param.18) | copy-start | bytes 388
  1.8 7.3 %collective-permute-start.1 = (f32[32,1,256]{2,1,0:T(1,128)S(1)}, f32[32,1,256]{2,1,0:T(1,128)S(1)}, u32[]{:S(2)}, u32[]{:S(2)}) collective-permute-start(f32[32,1,256]{2,1,0:T(1,128)S(1)} %get-tuple-element.213), channel_id=1, source_target_pairs={{8,0},{16,8},{24,16},{0,24},{9,1},{17,9},{25,17},{1,25},{10,2},{18... | collective-permute-start | bytes 98312 | tf_op jit(solution)/shard_map/ppermute | solution.py:20
  6.9 5.7 collective-permute-start
  6.9 106.9 %copy-start.21 = (s32[2048]{0:T(1024)}, s32[2048]{0:T(1024)S(1)}, u32[]{:S(2)}) copy-start(s32[2048]{0:T(1024)S(1)} %iota_add_fusion) | copy-start | bytes 24580
  6.9 106.9 %copy-start.24 = (pred[2048]{0:T(1024)(128)(4,1)}, pred[2048]{0:T(1024)(128)(4,1)S(1)}, u32[]{:S(2)}) copy-start(pred[2048]{0:T(1024)(128)(4,1)S(1)} %iota_compare_fusion) | copy-start | bytes 6148
  12.9 6.7 %collective-permute-start.3 = (f32[32,10,1]{2,1,0:T(8,128)S(1)}, f32[32,10,1]{2,1,0:T(8,128)S(1)}, u32[]{:S(2)}, u32[]{:S(2)}) collective-permute-start(f32[32,10,1]{2,1,0:T(8,128)S(1)} %get-tuple-element.209), channel_id=1, source_target_pairs={{1,0},{2,1},{3,2},{4,3},{5,4},{6,5},{7,6},{0,7},{9,8},{10,9},{11,1... | collective-permute-start | bytes 3848 | tf_op jit(solution)/shard_map/ppermute | solution.py:20
  13.4 9.2 %collective-permute-start.2 = (f32[32,10,1]{2,1,0:T(8,128)S(1)}, f32[32,10,1]{2,1,0:T(8,128)S(1)}, u32[]{:S(2)}, u32[]{:S(2)}) collective-permute-start(f32[32,10,1]{2,1,0:T(8,128)S(1)} %get-tuple-element.208), channel_id=1, source_target_pairs={{0,1},{1,2},{2,3},{3,4},{4,5},{5,6},{6,7},{7,0},{8,9},{9,10},{10,1... | collective-permute-start | bytes 3848 | tf_op jit(solution)/shard_map/ppermute | solution.py:17
  13.4 296.4 %copy-start.26 = (pred[10]{0:T(512)(128)(4,1)}, pred[10]{0:T(512)(128)(4,1)S(1)}, u32[]{:S(2)}) copy-start(pred[10]{0:T(512)(128)(4,1)S(1)} %and_or_fusion) | copy-start | bytes 34
  13.5 100.4 %copy-start.29 = (f32[8]{0:T(128)}, f32[8]{0:T(128)S(1)}, u32[]{:S(2)}) copy-start(f32[8]{0:T(128)S(1)} %neg.2118) | copy-start | bytes 100
  13.5 100.4 %copy-start.30 = (f32[8]{0:T(128)}, f32[8]{0:T(128)S(1)}, u32[]{:S(2)}) copy-start(f32[8]{0:T(128)S(1)} %neg.2119) | copy-start | bytes 100
  24.2 13.4 %all-to-all-start = ((f32[2,32,8,256]{3,2,0,1:T(8,128)}), f32[2,32,8,256]{3,2,0,1:T(8,128)S(1)}, u32[]{:S(2)}, u32[]{:S(2)}) async-start(f32[2,32,8,256]{3,2,0,1:T(8,128)} %pad_maximum_fusion.3), calls=%async_computation | async-start | bytes 1048576 | tf_op jit(solution)/shard_map/all_to_all | solution.py:58
  28.2 85.7 %copy-start.20 = (f32[8,2048]{1,0:T(8,128)}, f32[8,2048]{1,0:T(8,128)S(1)}, u32[]{:S(2)}) copy-start(f32[8,2048]{1,0:T(8,128)S(1)} %fusion.44) | copy-start | bytes 196612
  196.3 21.7 %copy-start.32 = (s32[32]{0:T(128)S(1)}, s32[32]{0:T(128)}, u32[]{:S(2)}) copy-start(s32[32]{0:T(128)} %param.19) | copy-start | bytes 388
  196.3 53.7 %copy-start.1 = (f32[32,8,256]{2,1,0:T(8,128)S(1)}, f32[32,8,256]{2,1,0:T(8,128)}, u32[]{:S(2)}) copy-start(f32[32,8,256]{2,1,0:T(8,128)} %param.11) | copy-start | bytes 786436
  196.3 53.7 %copy-start.2 = (f32[32,8,256]{2,1,0:T(8,128)S(1)}, f32[32,8,256]{2,1,0:T(8,128)}, u32[]{:S(2)}) copy-start(f32[32,8,256]{2,1,0:T(8,128)} %param.10) | copy-start | bytes 786436
  202.1 50.2 %copy-start.4 = (f32[32]{0:T(128)S(1)}, f32[32]{0:T(128)}, u32[]{:S(2)}) copy-start(f32[32]{0:T(128)} %param.16) | copy-start | bytes 388
  214.4 57.3 %copy-start = (f32[32,8,256]{2,1,0:T(8,128)S(1)}, f32[32,8,256]{2,1,0:T(8,128)}, u32[]{:S(2)}) copy-start(f32[32,8,256]{2,1,0:T(8,128)} %param.17) | copy-start | bytes 786436
  214.4 57.6 %copy-start.6 = (f32[32,8,256]{2,1,0:T(8,128)S(1)}, f32[32,8,256]{2,1,0:T(8,128)}, u32[]{:S(2)}) copy-start(f32[32,8,256]{2,1,0:T(8,128)} %param.12) | copy-start | bytes 786436
  214.4 13.3 %all-to-all-start.1 = ((f32[8,1,16384]{2,1,0:T(1,128)}), f32[8,1,16384]{2,1,0:T(1,128)S(1)}, u32[]{:S(2)}, u32[]{:S(2)}) async-start(f32[8,1,16384]{2,1,0:T(1,128)} %reshape.77), calls=%async_computation.1 | async-start | bytes 1048576 | tf_op jit(solution)/shard_map/all_to_all | solution.py:62
  218.1 74.3 %copy-start.23 = (pred[8]{0:T(512)(128)(4,1)}, pred[8]{0:T(512)(128)(4,1)S(1)}, u32[]{:S(2)}) copy-start(pred[8]{0:T(512)(128)(4,1)S(1)} %dynamic-slice_compare_fusion) | copy-start | bytes 28
  250.2 4.3 collective-permute-start.5
  250.6 6.1 %collective-permute-start.4 = (f32[2,32,1,256]{3,2,1,0:T(1,128)S(1)}, f32[2,32,1,256]{3,2,1,0:T(1,128)S(1)}, u32[]{:S(2)}, u32[]{:S(2)}) collective-permute-start(f32[2,32,1,256]{3,2,1,0:T(1,128)S(1)} %get-tuple-element.206), channel_id=1, source_target_pairs={{0,8},{8,16},{16,24},{24,0},{1,9},{9,17},{17,25},{25,1},{2,10},{10... | collective-permute-start | bytes 196616 | tf_op jit(solution)/shard_map/ppermute | solution.py:17
  257.2 11.9 %collective-permute-start.7 = (f32[2,32,10,1]{3,2,1,0:T(8,128)S(1)}, f32[2,32,10,1]{3,2,1,0:T(8,128)S(1)}, u32[]{:S(2)}, u32[]{:S(2)}) collective-permute-start(f32[2,32,10,1]{3,2,1,0:T(8,128)S(1)} %get-tuple-element.195), channel_id=1, source_target_pairs={{1,0},{2,1},{3,2},{4,3},{5,4},{6,5},{7,6},{0,7},{9,8},{10,9},{11,1... | collective-permute-start | bytes 7688 | tf_op jit(solution)/shard_map/ppermute | solution.py:20
  257.2 13.3 %collective-permute-start.6 = (f32[2,32,10,1]{3,2,1,0:T(8,128)S(1)}, f32[2,32,10,1]{3,2,1,0:T(8,128)S(1)}, u32[]{:S(2)}, u32[]{:S(2)}) collective-permute-start(f32[2,32,10,1]{3,2,1,0:T(8,128)S(1)} %get-tuple-element.194), channel_id=1, source_target_pairs={{0,1},{1,2},{2,3},{3,4},{4,5},{5,6},{6,7},{7,0},{8,9},{9,10},{10,1... | collective-permute-start | bytes 7688 | tf_op jit(solution)/shard_map/ppermute | solution.py:17
  294.5 29.2 %copy-start.7 = (f32[1,8,256]{2,1,0:T(8,128)}, f32[1,8,256]{2,1,0:T(8,128)S(1)}, u32[]{:S(2)}) copy-start(f32[1,8,256]{2,1,0:T(8,128)S(1)} %get-tuple-element.88) | copy-start | bytes 24580
  294.5 29.2 %copy-start.8 = (f32[1,8,256]{2,1,0:T(8,128)}, f32[1,8,256]{2,1,0:T(8,128)S(1)}, u32[]{:S(2)}) copy-start(f32[1,8,256]{2,1,0:T(8,128)S(1)} %get-tuple-element.89) | copy-start | bytes 24580
  294.5 29.2 %copy-start.9 = (f32[1,8,256]{2,1,0:T(8,128)}, f32[1,8,256]{2,1,0:T(8,128)S(1)}, u32[]{:S(2)}) copy-start(f32[1,8,256]{2,1,0:T(8,128)S(1)} %get-tuple-element.90) | copy-start | bytes 24580
  294.5 29.2 %copy-start.10 = (f32[1,8,256]{2,1,0:T(8,128)}, f32[1,8,256]{2,1,0:T(8,128)S(1)}, u32[]{:S(2)}) copy-start(f32[1,8,256]{2,1,0:T(8,128)S(1)} %get-tuple-element.91) | copy-start | bytes 24580
  294.5 29.2 %copy-start.11 = (f32[1,8,256]{2,1,0:T(8,128)}, f32[1,8,256]{2,1,0:T(8,128)S(1)}, u32[]{:S(2)}) copy-start(f32[1,8,256]{2,1,0:T(8,128)S(1)} %get-tuple-element.92) | copy-start | bytes 24580
  294.5 29.2 %copy-start.12 = (f32[1,8,256]{2,1,0:T(8,128)}, f32[1,8,256]{2,1,0:T(8,128)S(1)}, u32[]{:S(2)}) copy-start(f32[1,8,256]{2,1,0:T(8,128)S(1)} %get-tuple-element.93) | copy-start | bytes 24580
  294.5 29.2 %copy-start.13 = (f32[1,8,256]{2,1,0:T(8,128)}, f32[1,8,256]{2,1,0:T(8,128)S(1)}, u32[]{:S(2)}) copy-start(f32[1,8,256]{2,1,0:T(8,128)S(1)} %get-tuple-element.94) | copy-start | bytes 24580
  294.5 29.2 %copy-start.14 = (f32[1,8,256]{2,1,0:T(8,128)}, f32[1,8,256]{2,1,0:T(8,128)S(1)}, u32[]{:S(2)}) copy-start(f32[1,8,256]{2,1,0:T(8,128)S(1)} %get-tuple-element.95) | copy-start | bytes 24580
  294.5 29.2 %copy-start.15 = (f32[1,8,256]{2,1,0:T(8,128)}, f32[1,8,256]{2,1,0:T(8,128)S(1)}, u32[]{:S(2)}) copy-start(f32[1,8,256]{2,1,0:T(8,128)S(1)} %get-tuple-element.96) | copy-start | bytes 24580
  294.5 29.2 %copy-start.16 = (f32[1,8,256]{2,1,0:T(8,128)}, f32[1,8,256]{2,1,0:T(8,128)S(1)}, u32[]{:S(2)}) copy-start(f32[1,8,256]{2,1,0:T(8,128)S(1)} %get-tuple-element.97) | copy-start | bytes 24580
  294.5 29.2 %copy-start.17 = (f32[1,8,256]{2,1,0:T(8,128)}, f32[1,8,256]{2,1,0:T(8,128)S(1)}, u32[]{:S(2)}) copy-start(f32[1,8,256]{2,1,0:T(8,128)S(1)} %get-tuple-element.98) | copy-start | bytes 24580
  294.5 29.2 %copy-start.18 = (f32[1,8,256]{2,1,0:T(8,128)}, f32[1,8,256]{2,1,0:T(8,128)S(1)}, u32[]{:S(2)}) copy-start(f32[1,8,256]{2,1,0:T(8,128)S(1)} %get-tuple-element.99) | copy-start | bytes 24580
  294.6 29.2 %copy-start.19 = (f32[1,8,256]{2,1,0:T(8,128)}, f32[1,8,256]{2,1,0:T(8,128)S(1)}, u32[]{:S(2)}) copy-start(f32[1,8,256]{2,1,0:T(8,128)S(1)} %get-tuple-element.68) | copy-start | bytes 24580
  295.1 4.3 collective-permute-start.9
  295.5 5.7 collective-permute-start.8
  301.5 6.1 %collective-permute-start.11 = (f32[32,10,1]{2,1,0:T(8,128)S(1)}, f32[32,10,1]{2,1,0:T(8,128)S(1)}, u32[]{:S(2)}, u32[]{:S(2)}) collective-permute-start(f32[32,10,1]{2,1,0:T(8,128)S(1)} %get-tuple-element.205), channel_id=1, source_target_pairs={{1,0},{2,1},{3,2},{4,3},{5,4},{6,5},{7,6},{0,7},{9,8},{10,9},{11,1... | collective-permute-start | bytes 3848 | tf_op jit(solution)/shard_map/ppermute | solution.py:20
  301.5 8.3 %collective-permute-start.10 = (f32[32,10,1]{2,1,0:T(8,128)S(1)}, f32[32,10,1]{2,1,0:T(8,128)S(1)}, u32[]{:S(2)}, u32[]{:S(2)}) collective-permute-start(f32[32,10,1]{2,1,0:T(8,128)S(1)} %get-tuple-element.204), channel_id=1, source_target_pairs={{0,1},{1,2},{2,3},{3,4},{4,5},{5,6},{6,7},{7,0},{8,9},{9,10},{10,1... | collective-permute-start | bytes 3848 | tf_op jit(solution)/shard_map/ppermute | solution.py:17
  325.0 77.2 %copy-start.22 = (s32[2048]{0:T(1024)S(1)}, s32[2048]{0:T(1024)}, u32[]{:S(2)}) copy-start(s32[2048]{0:T(1024)} %copy-done.21) | copy-start | bytes 24580
  325.0 77.2 %copy-start.25 = (pred[2048]{0:T(1024)(128)(4,1)S(1)}, pred[2048]{0:T(1024)(128)(4,1)}, u32[]{:S(2)}) copy-start(pred[2048]{0:T(1024)(128)(4,1)} %copy-done.24) | copy-start | bytes 6148
  538.4 5.0 collective-permute-start.13
  538.7 6.1 %collective-permute-start.12 = (f32[2,32,1,256]{3,2,0,1:T(1,128)S(1)}, f32[2,32,1,256]{3,2,0,1:T(1,128)S(1)}, u32[]{:S(2)}, u32[]{:S(2)}) collective-permute-start(f32[2,32,1,256]{3,2,0,1:T(1,128)S(1)} %get-tuple-element.200), channel_id=1, source_target_pairs={{0,8},{8,16},{16,24},{24,0},{1,9},{9,17},{17,25},{25,1},{2,10},{10... | collective-permute-start | bytes 196616 | tf_op jit(solution)/shard_map/ppermute | solution.py:17
  545.2 12.1 %collective-permute-start.15 = (f32[2,32,10,1]{3,2,0,1:T(8,128)S(1)}, f32[2,32,10,1]{3,2,0,1:T(8,128)S(1)}, u32[]{:S(2)}, u32[]{:S(2)}) collective-permute-start(f32[2,32,10,1]{3,2,0,1:T(8,128)S(1)} %get-tuple-element.193), channel_id=1, source_target_pairs={{1,0},{2,1},{3,2},{4,3},{5,4},{6,5},{7,6},{0,7},{9,8},{10,9},{11,1... | collective-permute-start | bytes 7688 | tf_op jit(solution)/shard_map/ppermute | solution.py:20
  545.3 13.3 %collective-permute-start.14 = (f32[2,32,10,1]{3,2,0,1:T(8,128)S(1)}, f32[2,32,10,1]{3,2,0,1:T(8,128)S(1)}, u32[]{:S(2)}, u32[]{:S(2)}) collective-permute-start(f32[2,32,10,1]{3,2,0,1:T(8,128)S(1)} %get-tuple-element.192), channel_id=1, source_target_pairs={{0,1},{1,2},{2,3},{3,4},{4,5},{5,6},{6,7},{7,0},{8,9},{9,10},{10,1... | collective-permute-start | bytes 7688 | tf_op jit(solution)/shard_map/ppermute | solution.py:17
  (3 other events, 25.6 us)
where the time goes:
time: 589 us; the launch traced here: 585 us
  matrix products  318 us (54%)
  local copies, waits for them, and re-layouts  82 us (14%)
  waiting for transfers between devices  74.9 us (13%)
  other arithmetic  61.9 us (11%)
  blocking collectives  25.1 us (4%)
  starting transfers between devices  21.6 us (4%)
    dot_general x2, matrix products, transform_band(): jnp.einsum('vetc,cj->vetj', scaled, inverse, precision=lax.Precision.HIGH...  165 us
    dot_general x2, matrix products, transform_band(): jnp.einsum('vetj,jc->vetc', circles, forward, precision=lax.Precision.HIG...  153 us
    unnamed x129, local copies, waits for them, and re-layouts  50.8 us
    div x2, other arithmetic, column_solve(): prev_value = (rhs + below * prev_value) / pivot  41.1 us
    ppermute x8, waiting for transfers between devices, extended(): lax.ppermute(lax.slice_in_dim(block, 0, width, axis=dim), axis, backward)  39.1 us
    ppermute x8, waiting for transfers between devices, extended(): lax.ppermute(lax.slice_in_dim(block, block.shape[dim] - width, None, axis...  16.8 us
    all_to_all x3, local copies, waits for them, and re-layouts, transform_band(): lax.all_to_all(damped, 'lon', split_axis=3, concat_axis=1, tiled=True)  13.9 us
    all_to_all x1, blocking collectives, transform_band(): lax.all_to_all(damped, 'lon', split_axis=3, concat_axis=1, tiled=True)  12.8 us
  transfers between devices with their start and end apart: 18, of which 17 were waited for; matrix products, arithmetic and copies ran while one was open for 1% of the time, Pallas kernels for 0%

commit v1 on v0

--- a/solution.py
+++ b/solution.py
@@ -1,8 +1,13 @@
+import functools
 import math
 
+import ml_dtypes
+import numpy as np
 import jax
 import jax.numpy as jnp
 from jax import lax
+from jax.experimental import pallas as pl
+from jax.experimental.pallas import tpu as pltpu
 from jax.sharding import PartitionSpec as P
 
 SUBSTEPS = 2
@@ -101,7 +106,7 @@
     return (new_wind, new_pressure)
 
 
-def body(
+def wide_body(
     zonal_wind,
     merid_wind,
     vertical_wind,
@@ -139,6 +144,326 @@
     return (zonal_wind, merid_wind, vertical_wind, pressure)
 
 
+LANE = 128
+TILE = 2 * LANE
+
+
+def circle_tables(length):
+    blocks = length // LANE
+    half = blocks // 2
+    m = np.arange(LANE, dtype=np.float64)[:, None]
+    tables = np.zeros((half, TILE, TILE))
+    waves = np.zeros((half, TILE))
+    c = np.arange(LANE)[None, :]
+    low = np.where(c <= LANE // 2, np.cos(2 * np.pi * m * c / LANE), np.sin(2 * np.pi * m * (c - LANE // 2) / LANE))
+    low = low * np.where((c == 0) | (c == LANE // 2), np.sqrt(1.0 / LANE), np.sqrt(2.0 / LANE))
+    k2 = np.arange(LANE // 2)[None, :]
+    angle = 2 * np.pi * m * (half + blocks * k2) / length
+    mid = np.concatenate([np.cos(angle), np.sin(angle)], axis=1) * np.sqrt(2.0 / LANE)
+    tables[0, :LANE, :LANE] = low
+    tables[0, LANE:, LANE:] = mid
+    waves[0, :LANE] = blocks * np.where(c[0] <= LANE // 2, c[0], c[0] - LANE // 2)
+    waves[0, LANE:] = np.tile(half + blocks * k2[0], 2)
+    for k1 in range(1, half):
+        k = k1 + blocks * c
+        angle = 2 * np.pi * ((m * k) % length) / length
+        cos, sin = np.cos(angle) / np.sqrt(LANE), np.sin(angle) / np.sqrt(LANE)
+        tables[k1] = np.block([[cos, -sin], [sin, cos]])
+        waves[k1] = np.tile(np.minimum(k[0], length - k[0]), 2)
+    high = tables.astype(ml_dtypes.bfloat16)
+    rest = (tables - high.astype(np.float64)).astype(ml_dtypes.bfloat16)
+    scale = np.full((half, TILE), 2.0 / blocks)
+    scale[0] = 1.0 / blocks
+    rows = np.zeros((8, half * TILE), np.float32)
+    rows[0] = waves.reshape(-1)
+    rows[1] = (4.0 * np.sin(2 * np.pi * waves / length) ** 2).reshape(-1)
+    rows[2] = scale.reshape(-1)
+    return high, rest, rows
+
+
+def split_parts(value):
+    high = value.astype(jnp.bfloat16)
+    rest = (value - high.astype(jnp.float32)).astype(jnp.bfloat16)
+    return high, rest
+
+
+def three_products(value, high_table, rest_table, transposed):
+    high, rest = split_parts(value)
+    dims = (((1,), (1 if transposed else 0,)), ((), ()))
+    rows = value.shape[0]
+    both = lax.dot_general(jnp.concatenate([high, rest], axis=0), high_table, dims, preferred_element_type=jnp.float32)
+    corr = lax.dot_general(high, rest_table, dims, preferred_element_type=jnp.float32)
+    return both[:rows] + (both[rows:] + corr)
+
+
+def weighted(terms):
+    total = None
+    for coef, value in terms:
+        if abs(coef) < 1e-12:
+            continue
+        if abs(abs(coef) - 1.0) < 1e-12:
+            term = value
+        else:
+            term = abs(coef) * value
+        if total is None:
+            total = term if coef > 0 else -term
+        else:
+            total = total + term if coef > 0 else total - term
+    return total
+
+
+def coarse_forward(xs):
+    count = len(xs)
+    half = count // 2
+    even = {b: xs[b] + xs[count - b] for b in range(1, half)}
+    odd = {b: xs[b] - xs[count - b] for b in range(1, half)}
+    real, imag = [], {}
+    for k in range(half + 1):
+        ends = xs[0] + xs[half] if k % 2 == 0 else xs[0] - xs[half]
+        real.append(weighted([(1.0, ends)] + [(math.cos(2 * math.pi * b * k / count), even[b]) for b in range(1, half)]))
+    for k in range(1, half):
+        imag[k] = weighted([(-math.sin(2 * math.pi * b * k / count), odd[b]) for b in range(1, half)])
+    pairs = [(real[0], real[half])] + [(real[k], imag[k]) for k in range(1, half)]
+    return pairs
+
+
+def coarse_inverse(pairs):
+    half = len(pairs)
+    count = 2 * half
+    first, last = pairs[0]
+    xs = [None] * count
+    for b in range(half + 1):
+        ends = first + last if b % 2 == 0 else first - last
+        cos_part = weighted([(1.0, ends)] + [(math.cos(2 * math.pi * b * k / count), pairs[k][0]) for k in range(1, half)])
+        if b in (0, half):
+            xs[b] = cos_part
+        else:
+            sin_part = weighted([(-math.sin(2 * math.pi * b * k / count), pairs[k][1]) for k in range(1, half)])
+            xs[b] = cos_part + sin_part
+            xs[count - b] = cos_part - sin_part
+    return xs
+
+
+def to_spectrum(x_ref, high_ref, rest_ref, work_ref, spec_ref, bands, per_band, add_ref=None):
+    rows = x_ref.shape[1]
+    split = x_ref.shape[2] // LANE
+    for band in range(bands):
+        xs = [
+            x_ref[band * per_band + d, :, h * LANE:(h + 1) * LANE]
+            for d in range(per_band)
+            for h in range(split)
+        ]
+        for t, (left, right) in enumerate(coarse_forward(xs)):
+            work_ref[band * rows:(band + 1) * rows, t * TILE:t * TILE + LANE] = left
+            work_ref[band * rows:(band + 1) * rows, t * TILE + LANE:(t + 1) * TILE] = right
+    for t in range(high_ref.shape[0]):
+        cols = slice(t * TILE, (t + 1) * TILE)
+        value = three_products(work_ref[:, cols], high_ref[t], rest_ref[t], False)
+        if add_ref is not None:
+            value = value + add_ref[:, cols]
+        spec_ref[:, cols] = value
+
+
+def lat_diff(value):
+    count = value.shape[0]
+    row = lax.broadcasted_iota(jnp.int32, value.shape, 0)
+    upper = jnp.where(row == count - 1, 0.0, pltpu.roll(value, count - 1, 0))
+    lower = jnp.where(row == 0, 0.0, pltpu.roll(value, 1, 0))
+    return upper - lower
+
+
+def filter_rows(rows_ref, cols, cols_ref):
+    wave = rows_ref[0:1, cols]
+    limit = cols_ref[:, 2:3]
+    ratio = limit / jnp.maximum(wave, 1.0)
+    damped = jnp.logical_and(wave > limit, cols_ref[:, 3:4] > 0)
+    return jnp.where(damped, ratio * ratio, 1.0)
+
+
+def circle_blocks(work_ref, band, rows, half):
+    span = slice(band * rows, (band + 1) * rows)
+    pairs = [
+        (work_ref[span, t * TILE:t * TILE + LANE], work_ref[span, t * TILE + LANE:(t + 1) * TILE])
+        for t in range(half)
+    ]
+    return coarse_inverse(pairs)
+
+
+def put_blocks(out_ref, xs, band, per_band):
+    split = out_ref.shape[2] // LANE
+    for b, value in enumerate(xs):
+        out_ref[band * per_band + b // split, :, (b % split) * LANE:(b % split + 1) * LANE] = value
+
+
+def circle_diff(xs):
+    count = len(xs)
+    lane = lax.broadcasted_iota(jnp.int32, xs[0].shape, 1)
+    ahead = [pltpu.roll(x, LANE - 1, 1) for x in xs]
+    behind = [pltpu.roll(x, 1, 1) for x in xs]
+    out = []
+    for b in range(count):
+        nxt = jnp.where(lane == LANE - 1, ahead[(b + 1) % count], ahead[b])
+        prv = jnp.where(lane == 0, behind[(b - 1) % count], behind[b])
+        out.append(nxt - prv)
+    return out
+
+
+def spectral_terms(spec, rows_ref, cols_ref, cols):
+    zonal = cols_ref[:, 0:1]
+    merid = cols_ref[:, 1:2]
+    factor = filter_rows(rows_ref, cols, cols_ref) * rows_ref[2:3, cols]
+    smooth = factor * spec
+    v_part = -(merid * factor) * lat_diff(spec)
+    d_part = (zonal * zonal) * rows_ref[1:2, cols] * smooth + merid * lat_diff(v_part)
+    return smooth, v_part, d_part
+
+
+def divergence_kernel(bands, per_band, x_ref, high_ref, rest_ref, rows_ref, cols_ref, d_ref, spec_ref, work_ref):
+    half = high_ref.shape[0]
+    rows = x_ref.shape[1]
+    to_spectrum(x_ref, high_ref, rest_ref, work_ref, spec_ref, bands, per_band)
+    for t in range(half):
+        cols = slice(t * TILE, (t + 1) * TILE)
+        _, _, d_part = spectral_terms(spec_ref[:, cols], rows_ref, cols_ref, cols)
+        work_ref[:, cols] = three_products(d_part, high_ref[t], rest_ref[t], True)
+    for band in range(bands):
+        put_blocks(d_ref, circle_blocks(work_ref, band, rows, half), band, per_band)
+
+
+def final_kernel(bands, per_band, x_ref, old_ref, high_ref, rest_ref, rows_ref, cols_ref, d_ref, u_ref, v_ref, spec_ref, work_ref, q_ref, v_work_ref):
+    half = high_ref.shape[0]
+    rows = x_ref.shape[1]
+    lats = old_ref.shape[0]
+    to_spectrum(x_ref, high_ref, rest_ref, work_ref, spec_ref, bands, per_band, old_ref)
+    for t in range(half):
+        cols = slice(t * TILE, (t + 1) * TILE)
+        smooth, v_part, d_part = spectral_terms(spec_ref[:, cols], rows_ref, cols_ref, cols)
+        value = three_products(jnp.concatenate([d_part, smooth, v_part], axis=0), high_ref[t], rest_ref[t], True)
+        work_ref[:, cols] = value[:lats]
+        q_ref[:, cols] = value[lats:2 * lats]
+        v_work_ref[:, cols] = value[2 * lats:]
+    for band in range(bands):
+        put_blocks(d_ref, circle_blocks(work_ref, band, rows, half), band, per_band)
+        put_blocks(v_ref, circle_blocks(v_work_ref, band, rows, half), band, per_band)
+        zonal = cols_ref[band * rows:(band + 1) * rows, 0:1]
+        moved = circle_diff(circle_blocks(q_ref, band, rows, half))
+        put_blocks(u_ref, [-zonal * x for x in moved], band, per_band)
+
+
+def factor_columns(a_ref, s_ref, ratio_ref, inv_ref):
+    levels = s_ref.shape[0]
+    prev = jnp.zeros(s_ref.shape[1:], jnp.float32)
+    for level in range(levels):
+        alpha = a_ref[level]
+        below = alpha * s_ref[level]
+        above = alpha * s_ref[level + 1] if level + 1 < levels else jnp.zeros_like(below)
+        inv = 1.0 / (1.0 + below + above + below * prev)
+        prev = -above * inv
+        ratio_ref[level] = prev
+        inv_ref[level] = inv
+
+
+def solve_columns(a_ref, s_ref, w_ref, p_ref, base_ref, d_ref, ratio_ref, inv_ref, w_out, p_out):
+    levels = s_ref.shape[0]
+
+    def star(level):
+        return p_ref[level] - s_ref[level] * (base_ref[level] + d_ref[level])
+
+    here = star(0)
+    prev = jnp.zeros_like(here)
+    for level in range(levels):
+        alpha = a_ref[level]
+        p_out[level] = here
+        if level + 1 < levels:
+            nxt = star(level + 1)
+            rhs = w_ref[level] - alpha * (nxt - here)
+        else:
+            nxt = here
+            rhs = w_ref[level] + alpha * here
+        prev = (rhs + alpha * s_ref[level] * prev) * inv_ref[level]
+        w_out[level] = prev
+        here = nxt
+    upper = w_out[levels - 1]
+    for level in range(levels - 1, 0, -1):
+        lower = w_out[level - 1] - ratio_ref[level - 1] * upper
+        w_out[level - 1] = lower
+        p_out[level] = p_out[level] - s_ref[level] * (upper - lower)
+        upper = lower
+    p_out[0] = p_out[0] - s_ref[0] * upper
+
+
+def first_column_kernel(a_ref, s_ref, w_ref, p_ref, base_ref, d_ref, w_out, p_out, ratio_ref, inv_ref):
+    factor_columns(a_ref, s_ref, ratio_ref, inv_ref)
+    solve_columns(a_ref, s_ref, w_ref, p_ref, base_ref, d_ref, ratio_ref, inv_ref, w_out, p_out)
+
+
+def last_column_kernel(a_ref, s_ref, w_ref, p_ref, base_ref, d_ref, ratio_ref, inv_ref, u_ref, v_ref, du_ref, dv_ref, u_out, v_out, w_out, p_out):
+    u_out[...] = u_ref[...] + du_ref[...]
+    v_out[...] = v_ref[...] + dv_ref[...]
+    solve_columns(a_ref, s_ref, w_ref, p_ref, base_ref, d_ref, ratio_ref, inv_ref, w_out, p_out)
+
+
+def level_body(
+    tables,
+    zonal_wind,
+    merid_wind,
+    vertical_wind,
+    pressure,
+    zonal_coef,
+    merid_coef,
+    level_coef,
+    sound_coef,
+    cutoff,
+    filter_mask,
+):
+    high, rest, rows = (jnp.asarray(t) for t in tables)
+    bands = lax.axis_size("lat")
+    per_band = lax.axis_size("lon")
+    lats = cutoff.shape[0]
+    both = lax.all_gather(jnp.stack([zonal_coef, merid_coef], axis=1), "lat", axis=0, tiled=True)
+    cols = jnp.concatenate([both, cutoff.astype(jnp.float32)[:, None], filter_mask.astype(jnp.float32)[:, None]], axis=1)
+    zonal_rows = zonal_coef[None, :, None]
+    merid_rows = merid_coef[None, :, None]
+    u_pad = extended(zonal_wind, (("lon", 2),), 1)
+    v_pad = rim_fix(extended(merid_wind, (("lat", 1),), 1), 1)
+    base = zonal_rows * (u_pad[:, :, 2:] - u_pad[:, :, :-2]) + merid_rows * (v_pad[:, 2:] - v_pad[:, :-2])
+
+    def swap(block):
+        return lax.all_to_all(block, ("lat", "lon"), split_axis=0, concat_axis=0, tiled=True)
+
+    vmem = pl.BlockSpec(memory_space=pltpu.VMEM)
+    smem = pl.BlockSpec(memory_space=pltpu.SMEM)
+    block = jax.ShapeDtypeStruct(pressure.shape, jnp.float32)
+    flat = jax.ShapeDtypeStruct((lats, rows.shape[1]), jnp.float32)
+    scratch = pltpu.VMEM(flat.shape, jnp.float32)
+
+    div, spec = pl.pallas_call(
+        functools.partial(divergence_kernel, bands, per_band),
+        out_shape=(block, flat), in_specs=[vmem] * 5, out_specs=(vmem, vmem), scratch_shapes=[scratch],
+    )(swap(pressure), high, rest, rows, cols)
+    w_mid, p_mid, ratio, inv = pl.pallas_call(
+        first_column_kernel,
+        out_shape=(block,) * 4, in_specs=[smem] + [vmem] * 5, out_specs=(vmem,) * 4,
+    )(level_coef, sound_coef, vertical_wind, pressure, base, swap(div))
+    div, du, dv = pl.pallas_call(
+        functools.partial(final_kernel, bands, per_band),
+        out_shape=(block,) * 3, in_specs=[vmem] * 6, out_specs=(vmem,) * 3, scratch_shapes=[scratch] * 4,
+    )(swap(p_mid), spec, high, rest, rows, cols)
+    return pl.pallas_call(
+        last_column_kernel,
+        out_shape=(block,) * 4, in_specs=[smem] + [vmem] * 11, out_specs=(vmem,) * 4,
+    )(level_coef, sound_coef, w_mid, p_mid, base, swap(div), ratio, inv, zonal_wind, merid_wind, swap(du), swap(dv))
+
+
+def body(tables, *arrays):
+    pressure = arrays[3]
+    devices = lax.axis_size("lat") * lax.axis_size("lon")
+    fits = pressure.shape[0] == devices and pressure.shape[1] % 8 == 0 and pressure.shape[2] % LANE == 0
+    if fits:
+        return level_body(tables, *arrays)
+    return wide_body(*arrays)
+
+
 def solution(mesh):
     in_specs = (
         P(None, "lat", "lon"),
@@ -158,4 +483,10 @@
         P(None, "lat", "lon"),
         P(None, "lat", "lon"),
     )
-    return jax.shard_map(body, mesh=mesh, in_specs=in_specs, out_specs=out_specs, check_vma=False)
+
+    def whole(*arrays):
+        tables = circle_tables(arrays[0].shape[2])
+        step = jax.shard_map(functools.partial(body, tables), mesh=mesh, in_specs=in_specs, out_specs=out_specs, check_vma=False)
+        return step(*arrays)
+
+    return whole

time: 589 us -> 107 us (0.18)
  matrix products: 318 us -> 0 us
  local copies, waits for them, and re-layouts: 82 us -> 3.58 us
  waiting for transfers between devices: 74.9 us -> 9.43 us
  other arithmetic: 61.9 us -> 1.12 us
  blocking collectives: 25.1 us -> 63 us
  Pallas kernels: 0 us -> 12.7 us
  starting transfers between devices: 21.6 us -> 15.7 us
    dot_general x4 -> x0, matrix products: 318 us -> none  [the longest x2 165 us: transform_band(): jnp.einsum('vetc,cj->vetj', scaled, inverse, precision=lax.Precision.HIGH...]
    unnamed x129 -> x21, local copies, waits for them, and re-layouts: 50.8 us -> 2.76 us
    div x2 -> x0, other arithmetic: 41.1 us -> none  [column_solve(): prev_value = (rhs + below * prev_value) / pivot]
    ppermute x8 -> x2, waiting for transfers between devices: 39.1 us -> 0.01 us  [extended(): lax.ppermute(lax.slice_in_dim(block, 0, width, axis=dim), axis, backward)]
    all_to_all x2 -> x4, blocking collectives: 25.1 us -> 53.9 us  [swap(): lax.all_to_all(block, ('lat', 'lon'), split_axis=0, concat_axis=0, tiled=...]
    ppermute x8 -> x2, waiting for transfers between devices: 16.8 us -> 0.01 us  [extended(): lax.ppermute(lax.slice_in_dim(block, block.shape[dim] - width, None, axis...]
    all_to_all x7 -> x0, local copies, waits for them, and re-layouts: 15.5 us -> none  [the longest x3 13.9 us: transform_band(): lax.all_to_all(damped, 'lon', split_axis=3, concat_axis=1, tiled=True)]
    pallas_call x0 -> x4, Pallas kernels: none -> 12.7 us  [the longest x1 3.91 us: level_body(): pl.pallas_call(functools.partial(final_kernel, bands, per_band), out_shap...]
  transfers between devices with their start and end apart: 18 -> 6, of which waited for: 17 -> 1; matrix products, arithmetic and copies ran while one was open for 1% -> 2% of each run, Pallas kernels for 0% -> 3%
where the time goes in v1:
time: 107 us; the launch traced here: 106 us
  blocking collectives  63 us (59%)
  starting transfers between devices  15.7 us (15%)
  Pallas kernels  12.7 us (12%)
  waiting for transfers between devices  9.43 us (9%)
  local copies, waits for them, and re-layouts  3.58 us (3%)
  other arithmetic  1.12 us (1%)
    all_to_all x4, blocking collectives, swap(): lax.all_to_all(block, ('lat', 'lon'), split_axis=0, concat_axis=0, tiled=...  53.9 us
    all_to_all x2, starting transfers between devices, swap(): lax.all_to_all(block, ('lat', 'lon'), split_axis=0, concat_axis=0, tiled=...  9.92 us
    all_to_all x2, waiting for transfers between devices, swap(): lax.all_to_all(block, ('lat', 'lon'), split_axis=0, concat_axis=0, tiled=...  9.42 us
    all_gather x1, blocking collectives, level_body(): lax.all_gather(jnp.stack([zonal_coef, merid_coef], axis=1), 'lat', axis=0...  9.14 us
    ppermute x2, starting transfers between devices, extended(): lax.ppermute(lax.slice_in_dim(block, 0, width, axis=dim), axis, backward)  3.93 us
    pallas_call x1, Pallas kernels, level_body(): pl.pallas_call(functools.partial(final_kernel, bands, per_band), out_shap...  3.91 us
    pallas_call x1, Pallas kernels, level_body(): pl.pallas_call(functools.partial(divergence_kernel, bands, per_band), out...  3.47 us
    pallas_call x1, Pallas kernels, level_body(): pl.pallas_call(last_column_kernel, out_shape=(block,) * 4, in_specs=[smem...  2.77 us
  transfers between devices with their start and end apart: 6, of which 1 were waited for; matrix products, arithmetic and copies ran while one was open for 2% of the time, Pallas kernels for 3%

profile of v1, /device:TPU:0, one launch (start us, length us, event | category | flops | bytes accessed | tf_op | source)
XLA Modules:
  0.0 106.3 jit_solution(4280434350032385301)
XLA Ops:
  0.6 0.0 copy-start.1
  0.6 0.0 copy-start
  0.7 7.3 %all-to-all-start = ((f32[32,8,256]{2,1,0:T(8,128)}), f32[32,8,256]{2,1,0:T(8,128)S(1)}, u32[]{:S(2)}, u32[]{:S(2)}) async-start(f32[32,8,256]{2,1,0:T(8,128)} %p_ref.1), calls=%async_computation | async-start | bytes 524288 | tf_op jit(solution)/shard_map/all_to_all | solution.py:432
  8.0 0.0 copy-done.1
  8.1 1.8 %collective-permute-start.2 = (f32[32,1,256]{2,1,0:T(1,128)S(1)}, f32[32,1,256]{2,1,0:T(1,128)S(1)}, u32[]{:S(2)}, u32[]{:S(2)}) collective-permute-start(f32[32,1,256]{2,1,0:T(1,128)S(1)} %get-tuple-element.24), channel_id=1, source_target_pairs={{0,8},{8,16},{16,24},{24,0},{1,9},{9,17},{17,25},{25,1},{2,10},{10... | collective-permute-start | bytes 98312 | tf_op jit(solution)/shard_map/ppermute | solution.py:22
  9.9 2.1 %collective-permute-start.3 = (f32[32,1,256]{2,1,0:T(1,128)S(1)}, f32[32,1,256]{2,1,0:T(1,128)S(1)}, u32[]{:S(2)}, u32[]{:S(2)}) collective-permute-start(f32[32,1,256]{2,1,0:T(1,128)S(1)} %get-tuple-element.25), channel_id=1, source_target_pairs={{8,0},{16,8},{24,16},{0,24},{9,1},{17,9},{25,17},{1,25},{10,2},{18... | collective-permute-start | bytes 98312 | tf_op jit(solution)/shard_map/ppermute | solution.py:25
  11.9 0.0 copy-done
  11.9 0.1 fusion.4
  12.0 1.9 %collective-permute-start = (f32[32,8,1]{2,1,0:T(8,128)S(1)}, f32[32,8,1]{2,1,0:T(8,128)S(1)}, u32[]{:S(2)}, u32[]{:S(2)}) collective-permute-start(f32[32,8,1]{2,1,0:T(8,128)S(1)} %get-tuple-element.22), channel_id=1, source_target_pairs={{1,0},{2,1},{3,2},{4,3},{5,4},{6,5},{7,6},{0,7},{9,8},{10,9},{11,1... | collective-permute-start | bytes 3080 | tf_op jit(solution)/shard_map/ppermute | solution.py:25
  13.9 0.0 collective-permute-start.1
  13.9 0.0 copy-start.6
  13.9 0.0 copy-start.7
  13.9 0.7 copy-done.6
  14.6 0.0 copy-done.7
  14.6 9.1 %all-gather = f32[4,8,2]{1,2,0:T(2,128)S(1)} all-gather(f32[1,8,2]{1,2,0:T(2,128)S(1)} %maximum_bitcast_fusion), channel_id=1, replica_groups=mesh['lat'=4,'lon'=8] {'lat'}, dimensions={0}, use_global_device_ids=true | all-gather | bytes 320 | tf_op jit(solution)/shard_map/all_gather | solution.py:423
  23.7 0.0 copy-start.8
  23.7 0.0 copy-start.9
  23.7 0.1 reshape.11
  23.8 0.6 copy-done.8
  24.4 0.0 copy-done.9
  24.4 0.7 copy.22.cols_ref
  25.1 0.0 all-to-all-done.x_ref
  25.1 0.0 copy-start.2
  25.1 0.7 copy-done.2
  25.8 3.5 %shard_map.156 = (f32[32,8,256]{2,1,0:T(8,128)}, f32[32,2048]{1,0:T(8,128)}) custom-call(f32[32,8,256]{2,1,0:T(8,128)} %copy-done.2, bf16[8,256,256]{2,1,0:T(8,128)(2,1)} %constant.20.clone.high_ref, bf16[8,256,256]{2,1,0:T(8,128)(2,1)} %constant.21.clone.rest_ref, f32[8,2048]{1,0:T(8,128)} %constant.22.clone.rows_ref, f32[32,4]{1,0:T(8,128)} %copy.22.cols_ref), custom_call_target="tpu_custom_call" | custom-call | tf_op jit(solution)/shard_map/pallas_call | solution.py:440
  29.3 2.6 %all-to-all-start.1 = ((f32[32,8,256]{2,1,0:T(8,128)}), f32[32,8,256]{2,1,0:T(8,128)S(1)}, u32[]{:S(2)}, u32[]{:S(2)}) async-start(f32[32,8,256]{2,1,0:T(8,128)} %get-tuple-element.13), calls=%async_computation.1 | async-start | bytes 524288 | tf_op jit(solution)/shard_map/all_to_all | solution.py:432
  31.9 0.0 collective-permute-done.2
  31.9 0.0 collective-permute-done.3
  31.9 0.1 maximum_select_fusion
  32.1 0.0 collective-permute-done
  32.1 0.0 collective-permute-done.1
  32.1 0.9 fusion.1.base_ref
  33.0 9.4 %all-to-all-done.1.d_ref = f32[32,8,256]{2,1,0:T(8,128)S(1)} async-done(((f32[32,8,256]{2,1,0:T(8,128)}), f32[32,8,256]{2,1,0:T(8,128)S(1)}, u32[]{:S(2)}, u32[]{:S(2)}) %all-to-all-start.1) | async-done | bytes 262176 | tf_op jit(solution)/shard_map/all_to_all | solution.py:432
  42.5 0.0 copy-start.3
  42.5 0.7 copy-done.3
  43.2 2.5 %shard_map.157 = (f32[32,8,256]{2,1,0:T(8,128)}, f32[32,8,256]{2,1,0:T(8,128)}, f32[32,8,256]{2,1,0:T(8,128)}, f32[32,8,256]{2,1,0:T(8,128)}) custom-call(f32[32]{0:T(128)} %a_ref.3, f32[32,8,256]{2,1,0:T(8,128)} %s_ref.3, f32[32,8,256]{2,1,0:T(8,128)} %w_ref.1, f32[32,8,256]{2,1,0:T(8,128)} %p_ref.1, f32[32,8,256]{2,1,0:T(8,128)} %fusion.1.base_ref, ...), custom_call_target="tpu_custom_call" | custom-call | tf_op jit(solution)/shard_map/pallas_call | solution.py:444
  45.7 13.9 %all_to_all.30.x_ref = f32[32,8,256]{2,1,0:T(8,128)} all-to-all(f32[32,8,256]{2,1,0:T(8,128)} %get-tuple-element.15.p_ref), channel_id=1, replica_groups=mesh['lat'=4,'lon'=8] {'lat','lon'}, dimensions={0} | all-to-all | bytes 524288 | tf_op jit(solution)/shard_map/all_to_all | solution.py:432
  59.6 3.9 %shard_map.158 = (f32[32,8,256]{2,1,0:T(8,128)}, f32[32,8,256]{2,1,0:T(8,128)}, f32[32,8,256]{2,1,0:T(8,128)}) custom-call(f32[32,8,256]{2,1,0:T(8,128)} %all_to_all.30.x_ref, f32[32,2048]{1,0:T(8,128)} %get-tuple-element.16.old_ref, bf16[8,256,256]{2,1,0:T(8,128)(2,1)} %constant.20.clone.high_ref, bf16[8,256,256]{2,1,0:T(8,128)(2,1)} %constant.21.clone.rest_ref, ...), custom_call_target="tpu_custom_call" | custom-call | tf_op jit(solution)/shard_map/pallas_call | solution.py:448
  63.5 0.0 copy-start.5
  63.5 14.0 %all_to_all.31.d_ref = f32[32,8,256]{2,1,0:T(8,128)} all-to-all(f32[32,8,256]{2,1,0:T(8,128)} %get-tuple-element.17), channel_id=1, replica_groups=mesh['lat'=4,'lon'=8] {'lat','lon'}, dimensions={0} | all-to-all | bytes 524288 | tf_op jit(solution)/shard_map/all_to_all | solution.py:432
  77.5 0.0 copy-done.5
  77.5 0.0 copy-start.4
  77.5 13.1 %all_to_all.32.du_ref = f32[32,8,256]{2,1,0:T(8,128)} all-to-all(f32[32,8,256]{2,1,0:T(8,128)S(1)} %copy-done.5), channel_id=1, replica_groups=mesh['lat'=4,'lon'=8] {'lat','lon'}, dimensions={0} | all-to-all | bytes 524288 | tf_op jit(solution)/shard_map/all_to_all | solution.py:432
  90.5 0.0 copy-done.4
  90.5 12.9 %all_to_all.33.dv_ref = f32[32,8,256]{2,1,0:T(8,128)} all-to-all(f32[32,8,256]{2,1,0:T(8,128)S(1)} %copy-done.4), channel_id=1, replica_groups=mesh['lat'=4,'lon'=8] {'lat','lon'}, dimensions={0} | all-to-all | bytes 524288 | tf_op jit(solution)/shard_map/all_to_all | solution.py:432
  103.5 2.8 %shard_map.159 = (f32[32,8,256]{2,1,0:T(8,128)}, f32[32,8,256]{2,1,0:T(8,128)}, f32[32,8,256]{2,1,0:T(8,128)}, f32[32,8,256]{2,1,0:T(8,128)}) custom-call(f32[32]{0:T(128)} %a_ref.3, f32[32,8,256]{2,1,0:T(8,128)} %s_ref.3, f32[32,8,256]{2,1,0:T(8,128)} %get-tuple-element.14.w_ref, f32[32,8,256]{2,1,0:T(8,128)} %get-tuple-element.15.p_ref, ...), custom_call_target="tpu_custom_call" | custom-call | tf_op jit(solution)/shard_map/pallas_call | solution.py:452
  (6 shorter events, 0.1 us)
Async XLA Ops:
  0.6 7.4 %copy-start.1 = (f32[32,8,256]{2,1,0:T(8,128)S(1)}, f32[32,8,256]{2,1,0:T(8,128)}, u32[]{:S(2)}) copy-start(f32[32,8,256]{2,1,0:T(8,128)} %v_ref.1) | copy-start | bytes 786436
  0.6 11.3 %copy-start = (f32[32,8,256]{2,1,0:T(8,128)S(1)}, f32[32,8,256]{2,1,0:T(8,128)}, u32[]{:S(2)}) copy-start(f32[32,8,256]{2,1,0:T(8,128)} %u_ref.1) | copy-start | bytes 786436
  0.7 24.5 %all-to-all-start = ((f32[32,8,256]{2,1,0:T(8,128)}), f32[32,8,256]{2,1,0:T(8,128)S(1)}, u32[]{:S(2)}, u32[]{:S(2)}) async-start(f32[32,8,256]{2,1,0:T(8,128)} %p_ref.1), calls=%async_computation | async-start | bytes 524288 | tf_op jit(solution)/shard_map/all_to_all | solution.py:432
  8.1 23.9 %collective-permute-start.2 = (f32[32,1,256]{2,1,0:T(1,128)S(1)}, f32[32,1,256]{2,1,0:T(1,128)S(1)}, u32[]{:S(2)}, u32[]{:S(2)}) collective-permute-start(f32[32,1,256]{2,1,0:T(1,128)S(1)} %get-tuple-element.24), channel_id=1, source_target_pairs={{0,8},{8,16},{16,24},{24,0},{1,9},{9,17},{17,25},{25,1},{2,10},{10... | collective-permute-start | bytes 98312 | tf_op jit(solution)/shard_map/ppermute | solution.py:22
  9.9 22.0 %collective-permute-start.3 = (f32[32,1,256]{2,1,0:T(1,128)S(1)}, f32[32,1,256]{2,1,0:T(1,128)S(1)}, u32[]{:S(2)}, u32[]{:S(2)}) collective-permute-start(f32[32,1,256]{2,1,0:T(1,128)S(1)} %get-tuple-element.25), channel_id=1, source_target_pairs={{8,0},{16,8},{24,16},{0,24},{9,1},{17,9},{25,17},{1,25},{10,2},{18... | collective-permute-start | bytes 98312 | tf_op jit(solution)/shard_map/ppermute | solution.py:25
  12.0 20.0 %collective-permute-start = (f32[32,8,1]{2,1,0:T(8,128)S(1)}, f32[32,8,1]{2,1,0:T(8,128)S(1)}, u32[]{:S(2)}, u32[]{:S(2)}) collective-permute-start(f32[32,8,1]{2,1,0:T(8,128)S(1)} %get-tuple-element.22), channel_id=1, source_target_pairs={{1,0},{2,1},{3,2},{4,3},{5,4},{6,5},{7,6},{0,7},{9,8},{10,9},{11,1... | collective-permute-start | bytes 3080 | tf_op jit(solution)/shard_map/ppermute | solution.py:25
  13.9 18.2 %collective-permute-start.1 = (f32[32,8,1]{2,1,0:T(8,128)S(1)}, f32[32,8,1]{2,1,0:T(8,128)S(1)}, u32[]{:S(2)}, u32[]{:S(2)}) collective-permute-start(f32[32,8,1]{2,1,0:T(8,128)S(1)} %get-tuple-element.23), channel_id=1, source_target_pairs={{0,1},{1,2},{2,3},{3,4},{4,5},{5,6},{6,7},{7,0},{8,9},{9,10},{10,1... | collective-permute-start | bytes 3080 | tf_op jit(solution)/shard_map/ppermute | solution.py:22
  13.9 0.7 copy-start.6
  13.9 0.7 copy-start.7
  23.7 0.7 copy-start.8
  23.7 0.7 copy-start.9
  25.1 0.7 copy-start.2
  29.3 13.2 %all-to-all-start.1 = ((f32[32,8,256]{2,1,0:T(8,128)}), f32[32,8,256]{2,1,0:T(8,128)S(1)}, u32[]{:S(2)}, u32[]{:S(2)}) async-start(f32[32,8,256]{2,1,0:T(8,128)} %get-tuple-element.13), calls=%async_computation.1 | async-start | bytes 524288 | tf_op jit(solution)/shard_map/all_to_all | solution.py:432
  42.5 0.7 copy-start.3
  63.5 14.0 %copy-start.5 = (f32[32,8,256]{2,1,0:T(8,128)S(1)}, f32[32,8,256]{2,1,0:T(8,128)}, u32[]{:S(2)}) copy-start(f32[32,8,256]{2,1,0:T(8,128)} %get-tuple-element.20) | copy-start | bytes 786436
  77.5 13.1 %copy-start.4 = (f32[32,8,256]{2,1,0:T(8,128)S(1)}, f32[32,8,256]{2,1,0:T(8,128)}, u32[]{:S(2)}) copy-start(f32[32,8,256]{2,1,0:T(8,128)} %get-tuple-element.21) | copy-start | bytes 786436

commit v2 on v1

--- a/solution.py
+++ b/solution.py
@@ -174,10 +174,10 @@
     rest = (tables - high.astype(np.float64)).astype(ml_dtypes.bfloat16)
     scale = np.full((half, TILE), 2.0 / blocks)
     scale[0] = 1.0 / blocks
-    rows = np.zeros((8, half * TILE), np.float32)
-    rows[0] = waves.reshape(-1)
-    rows[1] = (4.0 * np.sin(2 * np.pi * waves / length) ** 2).reshape(-1)
-    rows[2] = scale.reshape(-1)
+    rows = np.zeros((half, 8, TILE), np.float32)
+    rows[:, 0] = waves
+    rows[:, 1] = 4.0 * np.sin(2 * np.pi * waves / length) ** 2
+    rows[:, 2] = scale
     return high, rest, rows
 
 
@@ -244,24 +244,30 @@
     return xs
 
 
-def to_spectrum(x_ref, high_ref, rest_ref, work_ref, spec_ref, bands, per_band, add_ref=None):
-    rows = x_ref.shape[1]
+def to_spectrum(x_ref, high_ref, rest_ref, work_ref, spec_ref, bands, per_band, accumulate):
     split = x_ref.shape[2] // LANE
-    for band in range(bands):
+
+    def one_band(band, carry):
         xs = [
             x_ref[band * per_band + d, :, h * LANE:(h + 1) * LANE]
             for d in range(per_band)
             for h in range(split)
         ]
         for t, (left, right) in enumerate(coarse_forward(xs)):
-            work_ref[band * rows:(band + 1) * rows, t * TILE:t * TILE + LANE] = left
-            work_ref[band * rows:(band + 1) * rows, t * TILE + LANE:(t + 1) * TILE] = right
+            work_ref[t, band, :, :LANE] = left
+            work_ref[t, band, :, LANE:] = right
+        return carry
+
+    lax.fori_loop(0, bands, one_band, 0)
     for t in range(high_ref.shape[0]):
-        cols = slice(t * TILE, (t + 1) * TILE)
-        value = three_products(work_ref[:, cols], high_ref[t], rest_ref[t], False)
-        if add_ref is not None:
-            value = value + add_ref[:, cols]
-        spec_ref[:, cols] = value
+        value = three_products(joined(work_ref[t]), high_ref[t], rest_ref[t], False)
+        if accumulate:
+            value = value + spec_ref[t]
+        spec_ref[t] = value
+
+
+def joined(value):
+    return value.reshape((value.shape[0] * value.shape[1], value.shape[2]))
 
 
 def lat_diff(value):
@@ -272,20 +278,8 @@
     return upper - lower
 
 
-def filter_rows(rows_ref, cols, cols_ref):
-    wave = rows_ref[0:1, cols]
-    limit = cols_ref[:, 2:3]
-    ratio = limit / jnp.maximum(wave, 1.0)
-    damped = jnp.logical_and(wave > limit, cols_ref[:, 3:4] > 0)
-    return jnp.where(damped, ratio * ratio, 1.0)
-
-
-def circle_blocks(work_ref, band, rows, half):
-    span = slice(band * rows, (band + 1) * rows)
-    pairs = [
-        (work_ref[span, t * TILE:t * TILE + LANE], work_ref[span, t * TILE + LANE:(t + 1) * TILE])
-        for t in range(half)
-    ]
+def circle_blocks(work_ref, band):
+    pairs = [(work_ref[t, band, :, :LANE], work_ref[t, band, :, LANE:]) for t in range(work_ref.shape[0])]
     return coarse_inverse(pairs)
 
 
@@ -308,46 +302,14 @@
     return out
 
 
-def spectral_terms(spec, rows_ref, cols_ref, cols):
-    zonal = cols_ref[:, 0:1]
-    merid = cols_ref[:, 1:2]
-    factor = filter_rows(rows_ref, cols, cols_ref) * rows_ref[2:3, cols]
+def spectral_terms(spec, factor, sines, coef_ref):
+    coefs = coef_ref[...]
+    zonal = joined(coefs[:, 0])[:, 0:1]
+    merid = joined(coefs[:, 1])[:, 0:1]
     smooth = factor * spec
     v_part = -(merid * factor) * lat_diff(spec)
-    d_part = (zonal * zonal) * rows_ref[1:2, cols] * smooth + merid * lat_diff(v_part)
+    d_part = (zonal * zonal) * sines * smooth + merid * lat_diff(v_part)
     return smooth, v_part, d_part
-
-
-def divergence_kernel(bands, per_band, x_ref, high_ref, rest_ref, rows_ref, cols_ref, d_ref, spec_ref, work_ref):
-    half = high_ref.shape[0]
-    rows = x_ref.shape[1]
-    to_spectrum(x_ref, high_ref, rest_ref, work_ref, spec_ref, bands, per_band)
-    for t in range(half):
-        cols = slice(t * TILE, (t + 1) * TILE)
-        _, _, d_part = spectral_terms(spec_ref[:, cols], rows_ref, cols_ref, cols)
-        work_ref[:, cols] = three_products(d_part, high_ref[t], rest_ref[t], True)
-    for band in range(bands):
-        put_blocks(d_ref, circle_blocks(work_ref, band, rows, half), band, per_band)
-
-
-def final_kernel(bands, per_band, x_ref, old_ref, high_ref, rest_ref, rows_ref, cols_ref, d_ref, u_ref, v_ref, spec_ref, work_ref, q_ref, v_work_ref):
-    half = high_ref.shape[0]
-    rows = x_ref.shape[1]
-    lats = old_ref.shape[0]
-    to_spectrum(x_ref, high_ref, rest_ref, work_ref, spec_ref, bands, per_band, old_ref)
-    for t in range(half):
-        cols = slice(t * TILE, (t + 1) * TILE)
-        smooth, v_part, d_part = spectral_terms(spec_ref[:, cols], rows_ref, cols_ref, cols)
-        value = three_products(jnp.concatenate([d_part, smooth, v_part], axis=0), high_ref[t], rest_ref[t], True)
-        work_ref[:, cols] = value[:lats]
-        q_ref[:, cols] = value[lats:2 * lats]
-        v_work_ref[:, cols] = value[2 * lats:]
-    for band in range(bands):
-        put_blocks(d_ref, circle_blocks(work_ref, band, rows, half), band, per_band)
-        put_blocks(v_ref, circle_blocks(v_work_ref, band, rows, half), band, per_band)
-        zonal = cols_ref[band * rows:(band + 1) * rows, 0:1]
-        moved = circle_diff(circle_blocks(q_ref, band, rows, half))
-        put_blocks(u_ref, [-zonal * x for x in moved], band, per_band)
 
 
 def factor_columns(a_ref, s_ref, ratio_ref, inv_ref):
@@ -392,15 +354,180 @@
     p_out[0] = p_out[0] - s_ref[0] * upper
 
 
-def first_column_kernel(a_ref, s_ref, w_ref, p_ref, base_ref, d_ref, w_out, p_out, ratio_ref, inv_ref):
-    factor_columns(a_ref, s_ref, ratio_ref, inv_ref)
-    solve_columns(a_ref, s_ref, w_ref, p_ref, base_ref, d_ref, ratio_ref, inv_ref, w_out, p_out)
-
-
-def last_column_kernel(a_ref, s_ref, w_ref, p_ref, base_ref, d_ref, ratio_ref, inv_ref, u_ref, v_ref, du_ref, dv_ref, u_out, v_out, w_out, p_out):
-    u_out[...] = u_ref[...] + du_ref[...]
-    v_out[...] = v_ref[...] + dv_ref[...]
-    solve_columns(a_ref, s_ref, w_ref, p_ref, base_ref, d_ref, ratio_ref, inv_ref, w_out, p_out)
+def base_divergence(u_ref, v_ref, own_ref, west_ref, east_ref, south_ref, north_ref, base_ref, is_first, is_last):
+    zonal = own_ref[0][:, 0:1]
+    merid = own_ref[1][:, 0:1]
+    rows, width = u_ref.shape[1:]
+    lane = lax.broadcasted_iota(jnp.int32, (rows, width), 1)
+    row = lax.broadcasted_iota(jnp.int32, (rows, width), 0)
+    keep_south = jnp.where(is_first, 0.0, 1.0)
+    keep_north = jnp.where(is_last, 0.0, 1.0)
+    west = west_ref[...]
+    east = east_ref[...]
+    for level in range(u_ref.shape[0]):
+        u = u_ref[level]
+        v = v_ref[level]
+        ahead = jnp.where(lane == width - 1, east[:, level:level + 1], pltpu.roll(u, width - 1, 1))
+        behind = jnp.where(lane == 0, west[:, level:level + 1], pltpu.roll(u, 1, 1))
+        upper = jnp.where(row == rows - 1, keep_north * north_ref[level:level + 1, :], pltpu.roll(v, rows - 1, 0))
+        lower = jnp.where(row == 0, keep_south * south_ref[level:level + 1, :], pltpu.roll(v, 1, 0))
+        base_ref[level] = zonal * (ahead - behind) + merid * (upper - lower)
+
+
+def pack_edges(u_ref, v_ref, first_col, last_col, first_row, last_row):
+    rows, width = u_ref.shape[1:]
+    lane = lax.broadcasted_iota(jnp.int32, (rows, LANE), 1)
+    first = jnp.zeros((rows, LANE), jnp.float32)
+    last = jnp.zeros((rows, LANE), jnp.float32)
+    for level in range(u_ref.shape[0]):
+        first = jnp.where(lane == level, u_ref[level, :, 0:1], first)
+        last = jnp.where(lane == level, u_ref[level, :, width - 1:width], last)
+        first_row[level:level + 1, :] = v_ref[level, 0:1, :]
+        last_row[level:level + 1, :] = v_ref[level, rows - 1:rows, :]
+    first_col[...] = first
+    last_col[...] = last
+
+
+def fused_kernel(
+    bands, per_band, a_ref, u_ref, v_ref, w_ref, p_ref, s_ref, own_ref, limit_ref, high_ref, rest_ref, rows_ref,
+    u_out, v_out, w_out, p_out,
+    x1, d1, x2, d2, ur, vr, ds1, ds2, us, vs, w_mid, p_mid, base, ratio, inv,
+    work, qwork, vwork, spec, factor, coefs, cols_send, cols_recv, rows_send, rows_recv,
+    send_sems, recv_sems, edge_send, edge_recv,
+):
+    count = bands * per_band
+    band_me = lax.axis_index("lat")
+    lon_me = lax.axis_index("lon")
+    me = band_me * per_band + lon_me
+    half = high_ref.shape[0]
+
+    def place(index):
+        return (index // per_band, index % per_band)
+
+    barrier = pltpu.get_barrier_semaphore()
+
+    def greet(i, carry):
+        pl.semaphore_signal(barrier, inc=1, device_id=place((me + i) % count), device_id_type=pl.DeviceIdType.MESH)
+        return carry
+
+    lax.fori_loop(1, count, greet, 0)
+    pack_edges(u_ref, v_ref, cols_send.at[0], cols_send.at[1], rows_send.at[0], rows_send.at[1])
+    pl.semaphore_wait(barrier, count - 1)
+
+    def send(source, target, sem, index):
+        pltpu.make_async_remote_copy(
+            src_ref=source.at[index], dst_ref=target.at[me], send_sem=send_sems.at[sem], recv_sem=recv_sems.at[sem],
+            device_id=place(index), device_id_type=pl.DeviceIdType.MESH,
+        ).start()
+
+    def scatter(source, target, sem):
+        def one(i, carry):
+            send(source, target, sem, (me + i) % count)
+            return carry
+
+        lax.fori_loop(1, count, one, 0)
+        target[me] = source[me]
+
+    def gathered(target, sem):
+        block = target.at[pl.ds(0, count - 1)]
+        pltpu.make_async_copy(block, block, recv_sems.at[sem]).wait()
+
+    def sent(source, sem):
+        block = source.at[pl.ds(0, count - 1)]
+        pltpu.make_async_copy(block, block, send_sems.at[sem]).wait()
+
+    scatter(p_ref, x1, 0)
+
+    coef_copies = []
+    for i in range(1, bands):
+        coef_copies.append(pltpu.make_async_remote_copy(
+            src_ref=own_ref, dst_ref=coefs.at[band_me], send_sem=send_sems.at[5 + i], recv_sem=recv_sems.at[5 + i],
+            device_id=((band_me + i) % bands, lon_me), device_id_type=pl.DeviceIdType.MESH,
+        ))
+    for copy in coef_copies:
+        copy.start()
+    coefs[band_me] = own_ref[...]
+    edge_copies = []
+    for side, step in ((0, -1), (1, 1)):
+        edge_copies.append(pltpu.make_async_remote_copy(
+            src_ref=cols_send.at[side], dst_ref=cols_recv.at[side], send_sem=edge_send.at[side], recv_sem=edge_recv.at[side],
+            device_id=(band_me, (lon_me + per_band + step) % per_band), device_id_type=pl.DeviceIdType.MESH,
+        ))
+        edge_copies.append(pltpu.make_async_remote_copy(
+            src_ref=rows_send.at[side], dst_ref=rows_recv.at[side], send_sem=edge_send.at[2 + side], recv_sem=edge_recv.at[2 + side],
+            device_id=((band_me + bands + step) % bands, lon_me), device_id_type=pl.DeviceIdType.MESH,
+        ))
+    for copy in edge_copies:
+        copy.start()
+
+    limit = limit_ref[:, 0:1]
+    for t in range(half):
+        wave = rows_ref[t, 0:1, :]
+        quotient = limit / jnp.maximum(wave, 1.0)
+        factor[t] = jnp.where(wave > limit, quotient * quotient, 1.0) * rows_ref[t, 2:3, :]
+
+    for copy in coef_copies:
+        copy.wait_recv()
+    gathered(x1, 0)
+    to_spectrum(x1, high_ref, rest_ref, work, spec, bands, per_band, False)
+    for t in range(half):
+        _, _, d_part = spectral_terms(spec[t], factor[t], rows_ref[t, 1:2, :], coefs)
+        work[t] = three_products(d_part, high_ref[t], rest_ref[t], True).reshape(work.shape[1:])
+
+    def first_back(band, carry):
+        put_blocks(ds1, circle_blocks(work, band), band, per_band)
+        return carry
+
+    lax.fori_loop(0, bands, first_back, 0)
+    scatter(ds1, d1, 1)
+
+    factor_columns(a_ref, s_ref, ratio, inv)
+    for copy in edge_copies:
+        copy.wait_recv()
+    base_divergence(
+        u_ref, v_ref, own_ref, cols_recv.at[1], cols_recv.at[0], rows_recv.at[1], rows_recv.at[0], base,
+        band_me == 0, band_me == bands - 1,
+    )
+    gathered(d1, 1)
+    solve_columns(a_ref, s_ref, w_ref, p_ref, base, d1, ratio, inv, w_mid, p_mid)
+    scatter(p_mid, x2, 2)
+    gathered(x2, 2)
+    to_spectrum(x2, high_ref, rest_ref, work, spec, bands, per_band, True)
+    lats = spec.shape[1]
+    for t in range(half):
+        smooth, v_part, d_part = spectral_terms(spec[t], factor[t], rows_ref[t, 1:2, :], coefs)
+        value = three_products(jnp.concatenate([d_part, smooth, v_part], axis=0), high_ref[t], rest_ref[t], True)
+        work[t] = value[:lats].reshape(work.shape[1:])
+        qwork[t] = value[lats:2 * lats].reshape(work.shape[1:])
+        vwork[t] = value[2 * lats:].reshape(work.shape[1:])
+
+    def second_back(band, carry):
+        put_blocks(ds2, circle_blocks(work, band), band, per_band)
+        return carry
+
+    lax.fori_loop(0, bands, second_back, 0)
+    scatter(ds2, d2, 3)
+
+    def winds_back(band, carry):
+        put_blocks(vs, circle_blocks(vwork, band), band, per_band)
+        zonal = coefs[band, 0][:, 0:1]
+        moved = circle_diff(circle_blocks(qwork, band))
+        put_blocks(us, [-zonal * x for x in moved], band, per_band)
+        return carry
+
+    lax.fori_loop(0, bands, winds_back, 0)
+    scatter(us, ur, 4)
+    scatter(vs, vr, 5)
+    gathered(d2, 3)
+    solve_columns(a_ref, s_ref, w_mid, p_mid, base, d2, ratio, inv, w_out, p_out)
+    gathered(ur, 4)
+    u_out[...] = u_ref[...] + ur[...]
+    gathered(vr, 5)
+    v_out[...] = v_ref[...] + vr[...]
+    for source, sem in ((p_ref, 0), (ds1, 1), (p_mid, 2), (ds2, 3), (us, 4), (vs, 5)):
+        sent(source, sem)
+    for copy in coef_copies + edge_copies:
+        copy.wait_send()
 
 
 def level_body(
@@ -417,48 +544,45 @@
     filter_mask,
 ):
     high, rest, rows = (jnp.asarray(t) for t in tables)
+    half = high.shape[0]
+    length = half * TILE
     bands = lax.axis_size("lat")
     per_band = lax.axis_size("lon")
     lats = cutoff.shape[0]
-    both = lax.all_gather(jnp.stack([zonal_coef, merid_coef], axis=1), "lat", axis=0, tiled=True)
-    cols = jnp.concatenate([both, cutoff.astype(jnp.float32)[:, None], filter_mask.astype(jnp.float32)[:, None]], axis=1)
-    zonal_rows = zonal_coef[None, :, None]
-    merid_rows = merid_coef[None, :, None]
-    u_pad = extended(zonal_wind, (("lon", 2),), 1)
-    v_pad = rim_fix(extended(merid_wind, (("lat", 1),), 1), 1)
-    base = zonal_rows * (u_pad[:, :, 2:] - u_pad[:, :, :-2]) + merid_rows * (v_pad[:, 2:] - v_pad[:, :-2])
-
-    def swap(block):
-        return lax.all_to_all(block, ("lat", "lon"), split_axis=0, concat_axis=0, tiled=True)
-
+    levels, lat_rows, width = pressure.shape
+    own = jnp.broadcast_to(jnp.stack([zonal_coef, merid_coef])[:, :, None], (2, lat_rows, LANE))
+    limit = jnp.where(filter_mask > 0, cutoff, length).astype(jnp.float32)
+    limit = jnp.broadcast_to(limit[:, None], (lats, LANE))
     vmem = pl.BlockSpec(memory_space=pltpu.VMEM)
     smem = pl.BlockSpec(memory_space=pltpu.SMEM)
     block = jax.ShapeDtypeStruct(pressure.shape, jnp.float32)
-    flat = jax.ShapeDtypeStruct((lats, rows.shape[1]), jnp.float32)
-    scratch = pltpu.VMEM(flat.shape, jnp.float32)
-
-    div, spec = pl.pallas_call(
-        functools.partial(divergence_kernel, bands, per_band),
-        out_shape=(block, flat), in_specs=[vmem] * 5, out_specs=(vmem, vmem), scratch_shapes=[scratch],
-    )(swap(pressure), high, rest, rows, cols)
-    w_mid, p_mid, ratio, inv = pl.pallas_call(
-        first_column_kernel,
-        out_shape=(block,) * 4, in_specs=[smem] + [vmem] * 5, out_specs=(vmem,) * 4,
-    )(level_coef, sound_coef, vertical_wind, pressure, base, swap(div))
-    div, du, dv = pl.pallas_call(
-        functools.partial(final_kernel, bands, per_band),
-        out_shape=(block,) * 3, in_specs=[vmem] * 6, out_specs=(vmem,) * 3, scratch_shapes=[scratch] * 4,
-    )(swap(p_mid), spec, high, rest, rows, cols)
+
+    def scratch(*shape):
+        return pltpu.VMEM(shape, jnp.float32)
+
+    field = scratch(*pressure.shape)
+    waves = scratch(half, bands, lat_rows, TILE)
+    flat = scratch(half, lats, TILE)
+    dma = pltpu.SemaphoreType.DMA
     return pl.pallas_call(
-        last_column_kernel,
-        out_shape=(block,) * 4, in_specs=[smem] + [vmem] * 11, out_specs=(vmem,) * 4,
-    )(level_coef, sound_coef, w_mid, p_mid, base, swap(div), ratio, inv, zonal_wind, merid_wind, swap(du), swap(dv))
+        functools.partial(fused_kernel, bands, per_band),
+        out_shape=(block,) * 4,
+        in_specs=[smem] + [vmem] * 10,
+        out_specs=(vmem,) * 4,
+        scratch_shapes=[field] * 15 + [waves] * 3 + [flat] * 2 + [
+            scratch(bands, 2, lat_rows, LANE),
+            scratch(2, lat_rows, LANE), scratch(2, lat_rows, LANE),
+            scratch(2, levels, width), scratch(2, levels, width),
+            dma((5 + bands,)), dma((5 + bands,)), dma((4,)), dma((4,)),
+        ],
+        compiler_params=pltpu.CompilerParams(collective_id=0, has_side_effects=True),
+    )(level_coef, zonal_wind, merid_wind, vertical_wind, pressure, sound_coef, own, limit, high, rest, rows)
 
 
 def body(tables, *arrays):
     pressure = arrays[3]
     devices = lax.axis_size("lat") * lax.axis_size("lon")
-    fits = pressure.shape[0] == devices and pressure.shape[1] % 8 == 0 and pressure.shape[2] % LANE == 0
+    fits = pressure.shape[0] == devices and pressure.shape[0] <= LANE and pressure.shape[1] % 8 == 0 and pressure.shape[2] % LANE == 0
     if fits:
         return level_body(tables, *arrays)
     return wide_body(*arrays)

time: 107 us -> 63.6 us (0.59)
  blocking collectives: 63 us -> 0 us
  Pallas kernels: 12.7 us -> 55.5 us
  starting transfers between devices: 15.7 us -> 0 us
  waiting for transfers between devices: 9.43 us -> 0 us
  local copies, waits for them, and re-layouts: 3.58 us -> 7.17 us
  other arithmetic: 1.12 us -> 0.01 us
    all_to_all x4 -> x0, blocking collectives: 53.9 us -> none  [swap(): lax.all_to_all(block, ('lat', 'lon'), split_axis=0, concat_axis=0, tiled=...]
    pallas_call x4 -> x1, Pallas kernels: 12.7 us -> 55.5 us  [level_body(): pl.pallas_call(functools.partial(fused_kernel, bands, per_band), out_shap...]
    all_to_all x2 -> x0, starting transfers between devices: 9.92 us -> none  [swap(): lax.all_to_all(block, ('lat', 'lon'), split_axis=0, concat_axis=0, tiled=...]
    all_to_all x2 -> x0, waiting for transfers between devices: 9.42 us -> none  [swap(): lax.all_to_all(block, ('lat', 'lon'), split_axis=0, concat_axis=0, tiled=...]
    all_gather x1 -> x0, blocking collectives: 9.14 us -> none  [level_body(): lax.all_gather(jnp.stack([zonal_coef, merid_coef], axis=1), 'lat', axis=0...]
    ppermute x4 -> x0, starting transfers between devices: 5.76 us -> none  [the longest x2 3.93 us: extended(): lax.ppermute(lax.slice_in_dim(block, 0, width, axis=dim), axis, backward)]
    unnamed x21 -> x18, local copies, waits for them, and re-layouts: 2.76 us -> 5.83 us
    broadcast_in_dim x0 -> x2, local copies, waits for them, and re-layouts: none -> 1.35 us  [the longest x1 0.67 us: level_body(): limit = jnp.broadcast_to(limit[:, None], (lats, LANE))]
  transfers between devices with their start and end apart: 6 -> 0, of which waited for: 1 -> 0; matrix products, arithmetic and copies ran while one was open for 2% -> 0% of each run, Pallas kernels for 3% -> 0%
where the time goes in v2:
time: 63.6 us; the launch traced here: 63.3 us
  Pallas kernels  55.5 us (87%)
  local copies, waits for them, and re-layouts  7.17 us (11%)
  between operations  0.67 us (1%)
    pallas_call x1, Pallas kernels, level_body(): pl.pallas_call(functools.partial(fused_kernel, bands, per_band), out_shap...  55.5 us
    unnamed x18, local copies, waits for them, and re-layouts  5.83 us

profile of v2, /device:TPU:0, one launch (start us, length us, event | category | flops | bytes accessed | tf_op | source)
XLA Modules:
  0.0 63.3 jit_solution(4736113371681427483)
XLA Ops:
  0.6 0.0 copy-start.5
  0.6 0.0 copy-start.6
  0.7 0.6 %copy-done.5 = s32[32]{0:T(128)S(1)} copy-done((s32[32]{0:T(128)S(1)}, s32[32]{0:T(128)}, u32[]{:S(2)}) %copy-start.5) | copy-done | bytes 152
  1.3 0.0 copy-done.6
  1.3 0.0 copy-start.3
  1.3 0.0 copy-start.4
  1.3 0.6 %copy-done.3 = f32[8]{0:T(128)S(1)} copy-done((f32[8]{0:T(128)S(1)}, f32[8]{0:T(128)}, u32[]{:S(2)}) %copy-start.3) | copy-done | bytes 56
  2.0 0.0 copy-done.4
  2.0 0.7 %broadcast_in_dim.8.own_ref = f32[2,8,128]{2,1,0:T(8,128)} broadcast(f32[2,8]{1,0:T(2,128)S(1)} %pad_maximum_fusion), dimensions={0,1} | broadcast | bytes 8256 | tf_op jit(solution)/shard_map/broadcast_in_dim | solution.py:553
  2.7 0.7 %broadcast_in_dim.18.limit_ref = f32[32,128]{1,0:T(8,128)} broadcast(f32[32]{0:T(128)S(1)} %fusion), dimensions={0} | broadcast | bytes 16512 | tf_op jit(solution)/shard_map/broadcast_in_dim | solution.py:555
  3.3 55.5 %shard_map.156 = (f32[32,8,256]{2,1,0:T(8,128)}, f32[32,8,256]{2,1,0:T(8,128)}, f32[32,8,256]{2,1,0:T(8,128)}, f32[32,8,256]{2,1,0:T(8,128)}) custom-call(f32[32]{0:T(128)} %a_ref.1, f32[32,8,256]{2,1,0:T(8,128)} %u_ref.1, f32[32,8,256]{2,1,0:T(8,128)} %v_ref.1, f32[32,8,256]{2,1,0:T(8,128)} %w_ref.1, f32[32,8,256]{2,1,0:T(8,128)} %p_ref.1, ...), custom_call_target="tpu_custom_call" | custom-call | tf_op jit(solution)/shard_map/pallas_call | solution.py:567
  58.8 0.0 copy-start.2
  58.8 1.7 %copy.21 = f32[32,8,256]{2,1,0:T(8,128)} copy(f32[32,8,256]{2,1,0:T(8,128)} %get-tuple-element.8) | data formatting | bytes 524288
  60.5 0.0 copy-done.2
  60.5 0.0 copy-start.1
  60.5 0.7 %copy.22 = f32[32,8,256]{2,1,0:T(8,128)} copy(f32[32,8,256]{2,1,0:T(8,128)S(1)} %copy-done.2) | data formatting | bytes 524288
  61.3 0.3 copy-done.1
  61.6 0.0 copy-start
  61.6 0.7 %copy.23 = f32[32,8,256]{2,1,0:T(8,128)} copy(f32[32,8,256]{2,1,0:T(8,128)S(1)} %copy-done.1) | data formatting | bytes 524288
  62.3 0.3 copy-done
  62.6 0.7 %copy.24 = f32[32,8,256]{2,1,0:T(8,128)} copy(f32[32,8,256]{2,1,0:T(8,128)S(1)} %copy-done) | data formatting | bytes 524288
  (2 shorter events, 0.0 us)
Async XLA Ops:
  0.6 0.7 %copy-start.5 = (s32[32]{0:T(128)S(1)}, s32[32]{0:T(128)}, u32[]{:S(2)}) copy-start(s32[32]{0:T(128)} %param.21) | copy-start | bytes 388
  0.6 0.7 %copy-start.6 = (s32[32]{0:T(128)S(1)}, s32[32]{0:T(128)}, u32[]{:S(2)}) copy-start(s32[32]{0:T(128)} %param.22) | copy-start | bytes 388
  1.3 0.7 %copy-start.3 = (f32[8]{0:T(128)S(1)}, f32[8]{0:T(128)}, u32[]{:S(2)}) copy-start(f32[8]{0:T(128)} %param.18) | copy-start | bytes 100
  1.3 0.7 %copy-start.4 = (f32[8]{0:T(128)S(1)}, f32[8]{0:T(128)}, u32[]{:S(2)}) copy-start(f32[8]{0:T(128)} %param.17) | copy-start | bytes 100
  58.8 1.7 %copy-start.2 = (f32[32,8,256]{2,1,0:T(8,128)S(1)}, f32[32,8,256]{2,1,0:T(8,128)}, u32[]{:S(2)}) copy-start(f32[32,8,256]{2,1,0:T(8,128)} %get-tuple-element.9) | copy-start | bytes 786436
  60.5 1.0 %copy-start.1 = (f32[32,8,256]{2,1,0:T(8,128)S(1)}, f32[32,8,256]{2,1,0:T(8,128)}, u32[]{:S(2)}) copy-start(f32[32,8,256]{2,1,0:T(8,128)} %get-tuple-element.10) | copy-start | bytes 786436
  61.6 1.0 %copy-start = (f32[32,8,256]{2,1,0:T(8,128)S(1)}, f32[32,8,256]{2,1,0:T(8,128)}, u32[]{:S(2)}) copy-start(f32[32,8,256]{2,1,0:T(8,128)} %get-tuple-element.11) | copy-start | bytes 786436

commit v3 on v2

--- a/solution.py
+++ b/solution.py
@@ -244,21 +244,21 @@
     return xs
 
 
-def to_spectrum(x_ref, high_ref, rest_ref, work_ref, spec_ref, bands, per_band, accumulate):
+def to_spectrum(x_ref, high_ref, rest_ref, work_ref, spec_ref, units, per_band, accumulate):
     split = x_ref.shape[2] // LANE
 
-    def one_band(band, carry):
+    def one_unit(unit, carry):
         xs = [
-            x_ref[band * per_band + d, :, h * LANE:(h + 1) * LANE]
+            x_ref[d * units + unit, :, h * LANE:(h + 1) * LANE]
             for d in range(per_band)
             for h in range(split)
         ]
         for t, (left, right) in enumerate(coarse_forward(xs)):
-            work_ref[t, band, :, :LANE] = left
-            work_ref[t, band, :, LANE:] = right
+            work_ref[t, unit, :, :LANE] = left
+            work_ref[t, unit, :, LANE:] = right
         return carry
 
-    lax.fori_loop(0, bands, one_band, 0)
+    lax.fori_loop(0, units, one_unit, 0)
     for t in range(high_ref.shape[0]):
         value = three_products(joined(work_ref[t]), high_ref[t], rest_ref[t], False)
         if accumulate:
@@ -270,23 +270,15 @@
     return value.reshape((value.shape[0] * value.shape[1], value.shape[2]))
 
 
-def lat_diff(value):
-    count = value.shape[0]
-    row = lax.broadcasted_iota(jnp.int32, value.shape, 0)
-    upper = jnp.where(row == count - 1, 0.0, pltpu.roll(value, count - 1, 0))
-    lower = jnp.where(row == 0, 0.0, pltpu.roll(value, 1, 0))
-    return upper - lower
-
-
 def circle_blocks(work_ref, band):
     pairs = [(work_ref[t, band, :, :LANE], work_ref[t, band, :, LANE:]) for t in range(work_ref.shape[0])]
     return coarse_inverse(pairs)
 
 
-def put_blocks(out_ref, xs, band, per_band):
+def put_blocks(out_ref, xs, unit, units):
     split = out_ref.shape[2] // LANE
     for b, value in enumerate(xs):
-        out_ref[band * per_band + b // split, :, (b % split) * LANE:(b % split + 1) * LANE] = value
+        out_ref[(b // split) * units + unit, :, (b % split) * LANE:(b % split + 1) * LANE] = value
 
 
 def circle_diff(xs):
@@ -302,14 +294,38 @@
     return out
 
 
-def spectral_terms(spec, factor, sines, coef_ref):
-    coefs = coef_ref[...]
-    zonal = joined(coefs[:, 0])[:, 0:1]
-    merid = joined(coefs[:, 1])[:, 0:1]
-    smooth = factor * spec
-    v_part = -(merid * factor) * lat_diff(spec)
-    d_part = (zonal * zonal) * sines * smooth + merid * lat_diff(v_part)
-    return smooth, v_part, d_part
+def filter_values(limit, wave, scale):
+    quotient = limit / jnp.maximum(wave, 1.0)
+    return jnp.where(wave > limit, quotient * quotient, 1.0) * scale
+
+
+def spectral_terms(spec_ref, t, units, rows_ref, own_ref, near_ref):
+    rows = own_ref.shape[1]
+    wave, sines, scale = rows_ref[t, 0:1, :], rows_ref[t, 1:2, :], rows_ref[t, 2:3, :]
+    zonal = own_ref[0, :, 0:1]
+    merid = own_ref[1, :, 0:1]
+    factor = filter_values(own_ref[2, :, 0:1], wave, scale)
+    south = near_ref[0, 1, rows - 1:rows, 0:1] * filter_values(near_ref[0, 2, rows - 1:rows, 0:1], wave, scale)
+    north = near_ref[1, 1, 0:1, 0:1] * filter_values(near_ref[1, 2, 0:1, 0:1], wave, scale)
+    row = lax.broadcasted_iota(jnp.int32, (rows, TILE), 0)
+    around = merid * factor
+    along = (zonal * zonal) * sines * factor
+    smooth, v_parts, d_parts = [], [], []
+    for l in range(units):
+        own = spec_ref[t, l * rows:(l + 1) * rows, :]
+        below = spec_ref[t, units * rows + 2 * l:units * rows + 2 * l + 2, :]
+        above = spec_ref[t, (units + 1) * rows + 2 * l:(units + 1) * rows + 2 * l + 2, :]
+        upper = jnp.where(row == rows - 1, above[0:1], pltpu.roll(own, rows - 1, 0))
+        lower = jnp.where(row == 0, below[1:2], pltpu.roll(own, 1, 0))
+        mid = -around * (upper - lower)
+        v_south = -south * (own[0:1] - below[0:1])
+        v_north = -north * (above[1:2] - own[rows - 1:rows])
+        upper = jnp.where(row == rows - 1, v_north, pltpu.roll(mid, rows - 1, 0))
+        lower = jnp.where(row == 0, v_south, pltpu.roll(mid, 1, 0))
+        smooth.append(factor * own)
+        v_parts.append(mid)
+        d_parts.append(along * own + merid * (upper - lower))
+    return smooth, v_parts, d_parts
 
 
 def factor_columns(a_ref, s_ref, ratio_ref, inv_ref):
@@ -388,136 +404,225 @@
     last_col[...] = last
 
 
+def pack_halo(source, low, high, units):
+    rows = source.shape[1]
+    for g in range(low.shape[0]):
+        for l in range(units):
+            low[g, 2 * l:2 * l + 2, :] = source[g * units + l, 0:2, :]
+            high[g, 2 * l:2 * l + 2, :] = source[g * units + l, rows - 2:rows, :]
+
+
+def own_coefs(zc_ref, mc_ref, cutoff_ref, mask_ref, own_ref, first_lat, unfiltered):
+    rows = own_ref.shape[1]
+    row = lax.broadcasted_iota(jnp.int32, own_ref.shape[1:], 0)
+    zonal = jnp.zeros(own_ref.shape[1:], jnp.float32)
+    merid = jnp.zeros(own_ref.shape[1:], jnp.float32)
+    limit = jnp.zeros(own_ref.shape[1:], jnp.int32)
+    for r in range(rows):
+        zonal = jnp.where(row == r, zc_ref[r], zonal)
+        merid = jnp.where(row == r, mc_ref[r], merid)
+        filtered = mask_ref[first_lat + r]
+        bound = filtered * cutoff_ref[first_lat + r] + (1 - filtered) * unfiltered
+        limit = jnp.where(row == r, bound, limit)
+    own_ref[0] = zonal
+    own_ref[1] = merid
+    own_ref[2] = limit.astype(jnp.float32)
+
+
 def fused_kernel(
-    bands, per_band, a_ref, u_ref, v_ref, w_ref, p_ref, s_ref, own_ref, limit_ref, high_ref, rest_ref, rows_ref,
+    bands, per_band, a_ref, zc_ref, mc_ref, cutoff_ref, mask_ref, u_ref, v_ref, w_ref, p_ref, s_ref, high_ref, rest_ref, rows_ref,
     u_out, v_out, w_out, p_out,
-    x1, d1, x2, d2, ur, vr, ds1, ds2, us, vs, w_mid, p_mid, base, ratio, inv,
-    work, qwork, vwork, spec, factor, coefs, cols_send, cols_recv, rows_send, rows_recv,
-    send_sems, recv_sems, edge_send, edge_recv,
+    d1, d2, ur, vr, ds1, ds2, us, vs, w_mid, p_mid, base, ratio, inv,
+    x1, x2, wide, work, qwork, vwork, spec, own_ref, near, cols_send, cols_recv, rows_send, rows_recv, low, high,
+    send_sems, recv_sems, edge_send, edge_recv, halo_send, halo_recv,
 ):
     count = bands * per_band
     band_me = lax.axis_index("lat")
     lon_me = lax.axis_index("lon")
     me = band_me * per_band + lon_me
     half = high_ref.shape[0]
-
-    def place(index):
-        return (index // per_band, index % per_band)
+    lat_rows = u_ref.shape[1]
+    units = u_ref.shape[0] // per_band
+    spread = units + 2
+    mesh_id = pl.DeviceIdType.MESH
+    is_first = band_me == 0
+    is_last = band_me == bands - 1
 
     barrier = pltpu.get_barrier_semaphore()
 
     def greet(i, carry):
-        pl.semaphore_signal(barrier, inc=1, device_id=place((me + i) % count), device_id_type=pl.DeviceIdType.MESH)
+        other = (me + i) % count
+        pl.semaphore_signal(barrier, inc=1, device_id=(other // per_band, other % per_band), device_id_type=mesh_id)
         return carry
 
     lax.fori_loop(1, count, greet, 0)
+    own_coefs(zc_ref, mc_ref, cutoff_ref, mask_ref, own_ref, band_me * lat_rows, half * TILE)
+    pack_halo(p_ref, low.at[0], high.at[0], units)
     pack_edges(u_ref, v_ref, cols_send.at[0], cols_send.at[1], rows_send.at[0], rows_send.at[1])
+
+    @pl.when(is_first)
+    def _():
+        near[0] = jnp.zeros(near.shape[1:], jnp.float32)
+        for d in range(per_band):
+            x1[d * spread + units] = jnp.zeros(x1.shape[1:], jnp.float32)
+            x2[d * spread + units] = jnp.zeros(x2.shape[1:], jnp.float32)
+
+    @pl.when(is_last)
+    def _():
+        near[1] = jnp.zeros(near.shape[1:], jnp.float32)
+        for d in range(per_band):
+            x1[d * spread + units + 1] = jnp.zeros(x1.shape[1:], jnp.float32)
+            x2[d * spread + units + 1] = jnp.zeros(x2.shape[1:], jnp.float32)
+
     pl.semaphore_wait(barrier, count - 1)
 
-    def send(source, target, sem, index):
-        pltpu.make_async_remote_copy(
-            src_ref=source.at[index], dst_ref=target.at[me], send_sem=send_sems.at[sem], recv_sem=recv_sems.at[sem],
-            device_id=place(index), device_id_type=pl.DeviceIdType.MESH,
-        ).start()
-
-    def scatter(source, target, sem):
+    def scatter(source, target, sem, stride):
         def one(i, carry):
-            send(source, target, sem, (me + i) % count)
+            g = (lon_me + i) % per_band
+            pltpu.make_async_remote_copy(
+                src_ref=source.at[pl.ds(g * units, units)], dst_ref=target.at[pl.ds(lon_me * stride, units)],
+                send_sem=send_sems.at[sem], recv_sem=recv_sems.at[sem],
+                device_id=(band_me, g), device_id_type=mesh_id,
+            ).start()
             return carry
 
-        lax.fori_loop(1, count, one, 0)
-        target[me] = source[me]
+        lax.fori_loop(1, per_band, one, 0)
+        for l in range(units):
+            target[lon_me * stride + l] = source[lon_me * units + l]
 
     def gathered(target, sem):
-        block = target.at[pl.ds(0, count - 1)]
+        block = target.at[pl.ds(0, (per_band - 1) * units)]
         pltpu.make_async_copy(block, block, recv_sems.at[sem]).wait()
 
     def sent(source, sem):
-        block = source.at[pl.ds(0, count - 1)]
+        block = source.at[pl.ds(0, (per_band - 1) * units)]
         pltpu.make_async_copy(block, block, send_sems.at[sem]).wait()
 
-    scatter(p_ref, x1, 0)
-
-    coef_copies = []
-    for i in range(1, bands):
-        coef_copies.append(pltpu.make_async_remote_copy(
-            src_ref=own_ref, dst_ref=coefs.at[band_me], send_sem=send_sems.at[5 + i], recv_sem=recv_sems.at[5 + i],
-            device_id=((band_me + i) % bands, lon_me), device_id_type=pl.DeviceIdType.MESH,
-        ))
-    for copy in coef_copies:
-        copy.start()
-    coefs[band_me] = own_ref[...]
+    def spread_halo(target, phase):
+        def one(source, slot, sem, other):
+            def step(i, carry):
+                g = (lon_me + i) % per_band
+                pltpu.make_async_remote_copy(
+                    src_ref=source.at[g], dst_ref=target.at[lon_me * spread + slot],
+                    send_sem=halo_send.at[sem], recv_sem=halo_recv.at[sem],
+                    device_id=(other, g), device_id_type=mesh_id,
+                ).start()
+                return carry
+
+            lax.fori_loop(0, per_band, step, 0)
+
+        @pl.when(jnp.logical_not(is_first))
+        def _():
+            one(low.at[phase], units + 1, 2 * phase, band_me - 1)
+
+        @pl.when(jnp.logical_not(is_last))
+        def _():
+            one(high.at[phase], units, 2 * phase + 1, band_me + 1)
+
+    def halo_wait(phase, sems, upward):
+        block = low.at[phase]
+
+        @pl.when(jnp.logical_not(is_first))
+        def _():
+            pltpu.make_async_copy(block, block, sems.at[2 * phase + (0 if upward else 1)]).wait()
+
+        @pl.when(jnp.logical_not(is_last))
+        def _():
+            pltpu.make_async_copy(block, block, sems.at[2 * phase + (1 if upward else 0)]).wait()
+
+    def coef_copy(step, side):
+        return pltpu.make_async_remote_copy(
+            src_ref=own_ref, dst_ref=near.at[side], send_sem=edge_send.at[4 + side], recv_sem=edge_recv.at[4 + side],
+            device_id=((band_me + bands + step) % bands, lon_me), device_id_type=mesh_id,
+        )
+
+    @pl.when(jnp.logical_not(is_first))
+    def _():
+        coef_copy(-1, 1).start()
+
+    @pl.when(jnp.logical_not(is_last))
+    def _():
+        coef_copy(1, 0).start()
+
+    scatter(p_ref, x1, 0, spread)
+    spread_halo(x1, 0)
+
     edge_copies = []
     for side, step in ((0, -1), (1, 1)):
         edge_copies.append(pltpu.make_async_remote_copy(
             src_ref=cols_send.at[side], dst_ref=cols_recv.at[side], send_sem=edge_send.at[side], recv_sem=edge_recv.at[side],
-            device_id=(band_me, (lon_me + per_band + step) % per_band), device_id_type=pl.DeviceIdType.MESH,
+            device_id=(band_me, (lon_me + per_band + step) % per_band), device_id_type=mesh_id,
         ))
         edge_copies.append(pltpu.make_async_remote_copy(
             src_ref=rows_send.at[side], dst_ref=rows_recv.at[side], send_sem=edge_send.at[2 + side], recv_sem=edge_recv.at[2 + side],
-            device_id=((band_me + bands + step) % bands, lon_me), device_id_type=pl.DeviceIdType.MESH,
+            device_id=((band_me + bands + step) % bands, lon_me), device_id_type=mesh_id,
         ))
     for copy in edge_copies:
         copy.start()
 
-    limit = limit_ref[:, 0:1]
+    @pl.when(jnp.logical_not(is_first))
+    def _():
+        coef_copy(1, 0).wait_recv()
+
+    @pl.when(jnp.logical_not(is_last))
+    def _():
+        coef_copy(-1, 1).wait_recv()
+
+    gathered(x1, 0)
+    halo_wait(0, halo_recv, False)
+    to_spectrum(x1, high_ref, rest_ref, wide, spec, spread, per_band, False)
     for t in range(half):
-        wave = rows_ref[t, 0:1, :]
-        quotient = limit / jnp.maximum(wave, 1.0)
-        factor[t] = jnp.where(wave > limit, quotient * quotient, 1.0) * rows_ref[t, 2:3, :]
-
-    for copy in coef_copies:
-        copy.wait_recv()
-    gathered(x1, 0)
-    to_spectrum(x1, high_ref, rest_ref, work, spec, bands, per_band, False)
-    for t in range(half):
-        _, _, d_part = spectral_terms(spec[t], factor[t], rows_ref[t, 1:2, :], coefs)
+        _, _, d_parts = spectral_terms(spec, t, units, rows_ref, own_ref, near)
+        d_part = jnp.concatenate(d_parts, axis=0)
         work[t] = three_products(d_part, high_ref[t], rest_ref[t], True).reshape(work.shape[1:])
 
-    def first_back(band, carry):
-        put_blocks(ds1, circle_blocks(work, band), band, per_band)
+    def first_back(unit, carry):
+        put_blocks(ds1, circle_blocks(work, unit), unit, units)
         return carry
 
-    lax.fori_loop(0, bands, first_back, 0)
-    scatter(ds1, d1, 1)
+    lax.fori_loop(0, units, first_back, 0)
+    scatter(ds1, d1, 1, units)
 
     factor_columns(a_ref, s_ref, ratio, inv)
     for copy in edge_copies:
         copy.wait_recv()
     base_divergence(
         u_ref, v_ref, own_ref, cols_recv.at[1], cols_recv.at[0], rows_recv.at[1], rows_recv.at[0], base,
-        band_me == 0, band_me == bands - 1,
+        is_first, is_last,
     )
     gathered(d1, 1)
     solve_columns(a_ref, s_ref, w_ref, p_ref, base, d1, ratio, inv, w_mid, p_mid)
-    scatter(p_mid, x2, 2)
+    scatter(p_mid, x2, 2, spread)
+    pack_halo(p_mid, low.at[1], high.at[1], units)
+    spread_halo(x2, 1)
     gathered(x2, 2)
-    to_spectrum(x2, high_ref, rest_ref, work, spec, bands, per_band, True)
-    lats = spec.shape[1]
+    halo_wait(1, halo_recv, False)
+    to_spectrum(x2, high_ref, rest_ref, wide, spec, spread, per_band, True)
+    lats = units * lat_rows
     for t in range(half):
-        smooth, v_part, d_part = spectral_terms(spec[t], factor[t], rows_ref[t, 1:2, :], coefs)
-        value = three_products(jnp.concatenate([d_part, smooth, v_part], axis=0), high_ref[t], rest_ref[t], True)
+        smooth, v_parts, d_parts = spectral_terms(spec, t, units, rows_ref, own_ref, near)
+        value = three_products(jnp.concatenate(d_parts + smooth + v_parts, axis=0), high_ref[t], rest_ref[t], True)
         work[t] = value[:lats].reshape(work.shape[1:])
         qwork[t] = value[lats:2 * lats].reshape(work.shape[1:])
         vwork[t] = value[2 * lats:].reshape(work.shape[1:])
 
     def second_back(band, carry):
-        put_blocks(ds2, circle_blocks(work, band), band, per_band)
+        put_blocks(ds2, circle_blocks(work, band), band, units)
         return carry
 
-    lax.fori_loop(0, bands, second_back, 0)
-    scatter(ds2, d2, 3)
+    lax.fori_loop(0, units, second_back, 0)
+    scatter(ds2, d2, 3, units)
 
     def winds_back(band, carry):
-        put_blocks(vs, circle_blocks(vwork, band), band, per_band)
-        zonal = coefs[band, 0][:, 0:1]
+        put_blocks(vs, circle_blocks(vwork, band), band, units)
+        zonal = own_ref[0, :, 0:1]
         moved = circle_diff(circle_blocks(qwork, band))
-        put_blocks(us, [-zonal * x for x in moved], band, per_band)
+        put_blocks(us, [-zonal * x for x in moved], band, units)
         return carry
 
-    lax.fori_loop(0, bands, winds_back, 0)
-    scatter(us, ur, 4)
-    scatter(vs, vr, 5)
+    lax.fori_loop(0, units, winds_back, 0)
+    scatter(us, ur, 4, units)
+    scatter(vs, vr, 5, units)
     gathered(d2, 3)
     solve_columns(a_ref, s_ref, w_mid, p_mid, base, d2, ratio, inv, w_out, p_out)
     gathered(ur, 4)
@@ -526,8 +631,18 @@
     v_out[...] = v_ref[...] + vr[...]
     for source, sem in ((p_ref, 0), (ds1, 1), (p_mid, 2), (ds2, 3), (us, 4), (vs, 5)):
         sent(source, sem)
-    for copy in coef_copies + edge_copies:
+    for phase in range(2):
+        halo_wait(phase, halo_send, True)
+    for copy in edge_copies:
         copy.wait_send()
+
+    @pl.when(jnp.logical_not(is_first))
+    def _():
+        coef_copy(-1, 1).wait_send()
+
+    @pl.when(jnp.logical_not(is_last))
+    def _():
+        coef_copy(1, 0).wait_send()
 
 
 def level_body(
@@ -545,14 +660,11 @@
 ):
     high, rest, rows = (jnp.asarray(t) for t in tables)
     half = high.shape[0]
-    length = half * TILE
     bands = lax.axis_size("lat")
     per_band = lax.axis_size("lon")
-    lats = cutoff.shape[0]
     levels, lat_rows, width = pressure.shape
-    own = jnp.broadcast_to(jnp.stack([zonal_coef, merid_coef])[:, :, None], (2, lat_rows, LANE))
-    limit = jnp.where(filter_mask > 0, cutoff, length).astype(jnp.float32)
-    limit = jnp.broadcast_to(limit[:, None], (lats, LANE))
+    units = levels // per_band
+    spread = units + 2
     vmem = pl.BlockSpec(memory_space=pltpu.VMEM)
     smem = pl.BlockSpec(memory_space=pltpu.SMEM)
     block = jax.ShapeDtypeStruct(pressure.shape, jnp.float32)
@@ -561,28 +673,34 @@
         return pltpu.VMEM(shape, jnp.float32)
 
     field = scratch(*pressure.shape)
-    waves = scratch(half, bands, lat_rows, TILE)
-    flat = scratch(half, lats, TILE)
+    arrivals = scratch(per_band * spread, lat_rows, width)
+    waves = scratch(half, units, lat_rows, TILE)
     dma = pltpu.SemaphoreType.DMA
     return pl.pallas_call(
         functools.partial(fused_kernel, bands, per_band),
         out_shape=(block,) * 4,
-        in_specs=[smem] + [vmem] * 10,
+        in_specs=[smem] * 5 + [vmem] * 8,
         out_specs=(vmem,) * 4,
-        scratch_shapes=[field] * 15 + [waves] * 3 + [flat] * 2 + [
-            scratch(bands, 2, lat_rows, LANE),
+        scratch_shapes=[field] * 13 + [arrivals] * 2 + [scratch(half, spread, lat_rows, TILE)] + [waves] * 3 + [
+            scratch(half, spread * lat_rows, TILE),
+            scratch(3, lat_rows, LANE), scratch(2, 3, lat_rows, LANE),
             scratch(2, lat_rows, LANE), scratch(2, lat_rows, LANE),
             scratch(2, levels, width), scratch(2, levels, width),
-            dma((5 + bands,)), dma((5 + bands,)), dma((4,)), dma((4,)),
+            scratch(2, per_band, lat_rows, width), scratch(2, per_band, lat_rows, width),
+            dma((6,)), dma((6,)), dma((6,)), dma((6,)), dma((4,)), dma((4,)),
         ],
         compiler_params=pltpu.CompilerParams(collective_id=0, has_side_effects=True),
-    )(level_coef, zonal_wind, merid_wind, vertical_wind, pressure, sound_coef, own, limit, high, rest, rows)
+    )(
+        level_coef, zonal_coef, merid_coef, cutoff, filter_mask,
+        zonal_wind, merid_wind, vertical_wind, pressure, sound_coef, high, rest, rows,
+    )
 
 
 def body(tables, *arrays):
     pressure = arrays[3]
-    devices = lax.axis_size("lat") * lax.axis_size("lon")
-    fits = pressure.shape[0] == devices and pressure.shape[0] <= LANE and pressure.shape[1] % 8 == 0 and pressure.shape[2] % LANE == 0
+    per_band = lax.axis_size("lon")
+    levels, lat_rows, width = pressure.shape
+    fits = lat_rows == 8 and levels == 4 * per_band and levels <= LANE and width % LANE == 0
     if fits:
         return level_body(tables, *arrays)
     return wide_body(*arrays)

time: 63.6 us -> 44.5 us (0.70)
  Pallas kernels: 55.5 us -> 39.1 us
  local copies, waits for them, and re-layouts: 7.17 us -> 4.5 us
    pallas_call x1, Pallas kernels: 55.5 us -> 39.1 us  [level_body(): pl.pallas_call(functools.partial(fused_kernel, bands, per_band), out_shap...]
    broadcast_in_dim x2 -> x0, local copies, waits for them, and re-layouts: 1.35 us -> none  [the longest x1 0.67 us: level_body(): limit = jnp.broadcast_to(limit[:, None], (lats, LANE))]
    unnamed x18 -> x10, local copies, waits for them, and re-layouts: 5.83 us -> 4.5 us
where the time goes in v3:
time: 44.5 us; the launch traced here: 44.2 us
  Pallas kernels  39.1 us (88%)
  local copies, waits for them, and re-layouts  4.5 us (10%)
  between operations  0.65 us (1%)
    pallas_call x1, Pallas kernels, level_body(): pl.pallas_call(functools.partial(fused_kernel, bands, per_band), out_shap...  39.1 us
    unnamed x10, local copies, waits for them, and re-layouts  4.5 us

profile of v3, /device:TPU:0, one launch (start us, length us, event | category | flops | bytes accessed | tf_op | source)
XLA Modules:
  0.0 44.2 jit_solution(6601908454031693000)
XLA Ops:
  0.6 39.1 %shard_map.156 = (f32[32,8,256]{2,1,0:T(8,128)}, f32[32,8,256]{2,1,0:T(8,128)}, f32[32,8,256]{2,1,0:T(8,128)}, f32[32,8,256]{2,1,0:T(8,128)}) custom-call(f32[32]{0:T(128)} %a_ref.1, f32[8]{0:T(128)} %zc_ref.1, f32[8]{0:T(128)} %mc_ref.1, s32[32]{0:T(128)} %cutoff_ref.1, s32[32]{0:T(128)} %mask_ref.1, f32[32,8,256]{2,1,0:T(8,128)} %u_ref.1, ...), custom_call_target="tpu_custom_call" | custom-call | tf_op jit(solution)/shard_map/pallas_call | solution.py:679
  39.7 0.0 copy-start.2
  39.7 1.7 %copy.21 = f32[32,8,256]{2,1,0:T(8,128)} copy(f32[32,8,256]{2,1,0:T(8,128)} %get-tuple-element.8) | data formatting | bytes 524288
  41.4 0.0 copy-done.2
  41.4 0.0 copy-start.1
  41.4 0.7 %copy.22 = f32[32,8,256]{2,1,0:T(8,128)} copy(f32[32,8,256]{2,1,0:T(8,128)S(1)} %copy-done.2) | data formatting | bytes 524288
  42.2 0.3 copy-done.1
  42.5 0.0 copy-start
  42.5 0.7 %copy.23 = f32[32,8,256]{2,1,0:T(8,128)} copy(f32[32,8,256]{2,1,0:T(8,128)S(1)} %copy-done.1) | data formatting | bytes 524288
  43.2 0.3 copy-done
  43.5 0.7 %copy.24 = f32[32,8,256]{2,1,0:T(8,128)} copy(f32[32,8,256]{2,1,0:T(8,128)S(1)} %copy-done) | data formatting | bytes 524288
Async XLA Ops:
  39.7 1.7 %copy-start.2 = (f32[32,8,256]{2,1,0:T(8,128)S(1)}, f32[32,8,256]{2,1,0:T(8,128)}, u32[]{:S(2)}) copy-start(f32[32,8,256]{2,1,0:T(8,128)} %get-tuple-element.9) | copy-start | bytes 786436
  41.4 1.0 %copy-start.1 = (f32[32,8,256]{2,1,0:T(8,128)S(1)}, f32[32,8,256]{2,1,0:T(8,128)}, u32[]{:S(2)}) copy-start(f32[32,8,256]{2,1,0:T(8,128)} %get-tuple-element.10) | copy-start | bytes 786436
  42.5 1.0 %copy-start = (f32[32,8,256]{2,1,0:T(8,128)S(1)}, f32[32,8,256]{2,1,0:T(8,128)}, u32[]{:S(2)}) copy-start(f32[32,8,256]{2,1,0:T(8,128)} %get-tuple-element.11) | copy-start | bytes 786436

commit v4 on v3

--- a/solution.py
+++ b/solution.py
@@ -430,11 +430,12 @@
 
 
 def fused_kernel(
-    bands, per_band, a_ref, zc_ref, mc_ref, cutoff_ref, mask_ref, u_ref, v_ref, w_ref, p_ref, s_ref, high_ref, rest_ref, rows_ref,
+    bands, per_band, a_ref, zc_ref, mc_ref, cutoff_ref, mask_ref, u_ref, v_ref, w_far, p_ref, s_far, high_far, rest_far, rows_ref,
     u_out, v_out, w_out, p_out,
     d1, d2, ur, vr, ds1, ds2, us, vs, w_mid, p_mid, base, ratio, inv,
     x1, x2, wide, work, qwork, vwork, spec, own_ref, near, cols_send, cols_recv, rows_send, rows_recv, low, high,
     send_sems, recv_sems, edge_send, edge_recv, halo_send, halo_recv,
+    w_ref, s_ref, high_ref, rest_ref, load_sems,
 ):
     count = bands * per_band
     band_me = lax.axis_index("lat")
@@ -448,6 +449,12 @@
     is_first = band_me == 0
     is_last = band_me == bands - 1
 
+    loads = [
+        pltpu.make_async_copy(far, here, load_sems.at[n])
+        for n, (far, here) in enumerate(((high_far, high_ref), (rest_far, rest_ref), (s_far, s_ref), (w_far, w_ref)))
+    ]
+    for load in loads:
+        load.start()
     barrier = pltpu.get_barrier_semaphore()
 
     def greet(i, carry):
@@ -568,6 +575,8 @@
     def _():
         coef_copy(-1, 1).wait_recv()
 
+    for load in loads:
+        load.wait()
     gathered(x1, 0)
     halo_wait(0, halo_recv, False)
     to_spectrum(x1, high_ref, rest_ref, wide, spec, spread, per_band, False)
@@ -667,6 +676,7 @@
     spread = units + 2
     vmem = pl.BlockSpec(memory_space=pltpu.VMEM)
     smem = pl.BlockSpec(memory_space=pltpu.SMEM)
+    far = pl.BlockSpec(memory_space=pl.ANY)
     block = jax.ShapeDtypeStruct(pressure.shape, jnp.float32)
 
     def scratch(*shape):
@@ -679,7 +689,7 @@
     return pl.pallas_call(
         functools.partial(fused_kernel, bands, per_band),
         out_shape=(block,) * 4,
-        in_specs=[smem] * 5 + [vmem] * 8,
+        in_specs=[smem] * 5 + [vmem] * 2 + [far, vmem, far, far, far, vmem],
         out_specs=(vmem,) * 4,
         scratch_shapes=[field] * 13 + [arrivals] * 2 + [scratch(half, spread, lat_rows, TILE)] + [waves] * 3 + [
             scratch(half, spread * lat_rows, TILE),
@@ -688,6 +698,7 @@
             scratch(2, levels, width), scratch(2, levels, width),
             scratch(2, per_band, lat_rows, width), scratch(2, per_band, lat_rows, width),
             dma((6,)), dma((6,)), dma((6,)), dma((6,)), dma((4,)), dma((4,)),
+            field, field, pltpu.VMEM(high.shape, high.dtype), pltpu.VMEM(rest.shape, rest.dtype), dma((4,)),
         ],
         compiler_params=pltpu.CompilerParams(collective_id=0, has_side_effects=True),
     )(

time: 44.5 us -> 43.7 us (0.982)
  Pallas kernels: 39.1 us -> 38.3 us
    pallas_call x1, Pallas kernels: 39.1 us -> 38.3 us  [level_body(): pl.pallas_call(functools.partial(fused_kernel, bands, per_band), out_shap...]
where the time goes in v4:
time: 43.7 us; the launch traced here: 43.4 us
  Pallas kernels  38.3 us (88%)
  local copies, waits for them, and re-layouts  4.5 us (10%)
  between operations  0.65 us (1%)
    pallas_call x1, Pallas kernels, level_body(): pl.pallas_call(functools.partial(fused_kernel, bands, per_band), out_shap...  38.3 us
    unnamed x10, local copies, waits for them, and re-layouts  4.5 us

profile of v4, /device:TPU:0, one launch (start us, length us, event | category | flops | bytes accessed | tf_op | source)
XLA Modules:
  0.0 43.4 jit_solution(13163800167617322367)
XLA Ops:
  0.6 38.3 %shard_map.156 = (f32[32,8,256]{2,1,0:T(8,128)}, f32[32,8,256]{2,1,0:T(8,128)}, f32[32,8,256]{2,1,0:T(8,128)}, f32[32,8,256]{2,1,0:T(8,128)}) custom-call(f32[32]{0:T(128)} %a_ref.1, f32[8]{0:T(128)} %zc_ref.1, f32[8]{0:T(128)} %mc_ref.1, s32[32]{0:T(128)} %cutoff_ref.1, s32[32]{0:T(128)} %mask_ref.1, f32[32,8,256]{2,1,0:T(8,128)} %u_ref.1, ...), custom_call_target="tpu_custom_call" | custom-call | tf_op jit(solution)/shard_map/pallas_call | solution.py:689
  38.9 0.0 copy-start.2
  38.9 1.7 %copy.21 = f32[32,8,256]{2,1,0:T(8,128)} copy(f32[32,8,256]{2,1,0:T(8,128)} %get-tuple-element.8) | data formatting | bytes 524288
  40.6 0.0 copy-done.2
  40.6 0.0 copy-start.1
  40.6 0.7 %copy.22 = f32[32,8,256]{2,1,0:T(8,128)} copy(f32[32,8,256]{2,1,0:T(8,128)S(1)} %copy-done.2) | data formatting | bytes 524288
  41.3 0.3 copy-done.1
  41.7 0.0 copy-start
  41.7 0.7 %copy.23 = f32[32,8,256]{2,1,0:T(8,128)} copy(f32[32,8,256]{2,1,0:T(8,128)S(1)} %copy-done.1) | data formatting | bytes 524288
  42.4 0.3 copy-done
  42.7 0.7 %copy.24 = f32[32,8,256]{2,1,0:T(8,128)} copy(f32[32,8,256]{2,1,0:T(8,128)S(1)} %copy-done) | data formatting | bytes 524288
Async XLA Ops:
  38.9 1.7 %copy-start.2 = (f32[32,8,256]{2,1,0:T(8,128)S(1)}, f32[32,8,256]{2,1,0:T(8,128)}, u32[]{:S(2)}) copy-start(f32[32,8,256]{2,1,0:T(8,128)} %get-tuple-element.9) | copy-start | bytes 786436
  40.6 1.0 %copy-start.1 = (f32[32,8,256]{2,1,0:T(8,128)S(1)}, f32[32,8,256]{2,1,0:T(8,128)}, u32[]{:S(2)}) copy-start(f32[32,8,256]{2,1,0:T(8,128)} %get-tuple-element.10) | copy-start | bytes 786436
  41.7 1.0 %copy-start = (f32[32,8,256]{2,1,0:T(8,128)S(1)}, f32[32,8,256]{2,1,0:T(8,128)}, u32[]{:S(2)}) copy-start(f32[32,8,256]{2,1,0:T(8,128)} %get-tuple-element.11) | copy-start | bytes 786436
